TPU v7x, 128 devices: a whole 4x4x4 slice. The times are simulated.
128 devices in a mesh: gx: 4 (over y), gy: 8 (over z, x_hi), gz: 4 (over x_lo, core).
Axes of the slice: x: 4 (x_hi: 2, x_lo: 2; x = x_hi * 2 + x_lo), y: 4, z: 4, core: 2. Of those that a mesh axis runs over, the one named last changes fastest.
Arguments:
- right_side: float32 [64, 1024, 1024], P('gz', 'gx', 'gy'), may hold values from -8 to 8
- diagonal: float32 [64, 1024, 1024], P('gz', 'gx', 'gy'), may hold values from 0.02 to 1
- regime: int32 [1024, 1024], P('gx', 'gy'), may hold values from 0 to 7
- inverses: float32 [8, 64, 64], replicated, as said below
Outputs:
- solution: float32 [64, 1024, 1024], P('gz', 'gx', 'gy')
- residual: float32 [64, 1024, 1024], P('gz', 'gx', 'gy')
Inputs may be any that keep to these rules, and one draw needn't show every extreme that they name: `inverses`: each block is symmetric positive definite.
All inputs are finite; a program needn't handle non-finite values.
Results may differ from a plain program's by a relative error of at most 0.00025.
Values sent between devices are 32-bit elements; how exact they have to be, the bound alone decides.
A program may use at most 128 MiB of HBM per device.

v0:
```python
import jax
import jax.numpy as jnp
from jax import lax
from jax.sharding import Mesh
from jax.sharding import PartitionSpec as P

NREG = 8
ITERS = 3
GX_GZ = ("gx", "gz_0", "gz_1")
GY = ("gy_0", "gy_1")
GZ = ("gz_0", "gz_1")
GX_GY_GZ = ("gx", "gy_0", "gy_1", "gz_0", "gz_1")


def extended(cells, sides, width):
    for axis, dim in sides:
        count = lax.axis_size(axis)
        ends = count - 1
        head = lax.slice_in_dim(cells, 0, width, axis=dim)
        tail = lax.slice_in_dim(cells, cells.shape[dim] - width, cells.shape[dim], axis=dim)
        cells = jnp.concatenate(
            [
                lax.ppermute(tail, axis, [(i, (i + 1) % count) for i in range(ends)]),
                cells,
                lax.ppermute(head, axis, [((i + 1) % count, i) for i in range(ends)]),
            ],
            axis=dim,
        )
    return cells


def over_axes(x, axes):
    for axis in axes:
        x = lax.psum(x, axis)
    return x


def sent_together(arrays, axis, split_dim, concat_dim, along):
    ends, at = ([], 0)
    for a in arrays[:-1]:
        at += a.shape[along]
        ends.append(at)
    both = jnp.concatenate(arrays, axis=along)
    return tuple(
        jnp.split(
            lax.all_to_all(both, axis, split_axis=split_dim, concat_axis=concat_dim, tiled=True),
            ends,
            axis=along,
        )
    )


def stencil(padded, grid_field, diagonal):
    beside = padded[2:, 1:-1, 1:-1] + padded[:-2, 1:-1, 1:-1]
    beside = beside + padded[1:-1, 2:, 1:-1] + padded[1:-1, :-2, 1:-1]
    beside = beside + padded[1:-1, 1:-1, 2:] + padded[1:-1, 1:-1, :-2]
    return (6.0 + diagonal) * grid_field - beside


def operate(grid_field, diagonal):
    flat_pad = extended(grid_field, ((GX_GZ, 1), (GY, 2)), 1)
    padded = jnp.pad(flat_pad, ((1, 1), (0, 0), (0, 0)))
    return stencil(padded, grid_field, diagonal)


def apply_blocks(matrices, flattened, chosen):
    result = jnp.zeros((matrices.shape[1], flattened.shape[1]), jnp.float32)
    for member in range(NREG):
        product = jnp.dot(matrices[member], flattened, precision=lax.Precision.HIGHEST)
        result = result + jnp.where(chosen[None, :] == member, product, jnp.zeros_like(product))
    return result


def precondition(grid_field, regime, inverses):
    layers = grid_field.shape[0]
    share_rows = grid_field.shape[1]
    offset = lax.axis_index(GZ) * share_rows
    chosen = lax.dynamic_slice_in_dim(regime, offset, share_rows, 0).reshape(-1)
    result = apply_blocks(inverses, grid_field.reshape(layers, -1), chosen)
    return result.reshape(grid_field.shape)


def paired(residual, precond, image):
    return (
        over_axes(jnp.sum(residual * precond), GX_GY_GZ),
        over_axes(jnp.sum(image * precond), GX_GY_GZ),
    )


def per_device(right_side, diagonal, regime, inverses):
    right_side, diagonal = (
        lax.all_to_all(right_side, GZ, split_axis=1, concat_axis=0, tiled=True),
        lax.all_to_all(diagonal, GZ, split_axis=1, concat_axis=0, tiled=True),
    )
    solution = jnp.zeros_like(right_side)
    residual = right_side
    precond = precondition(residual, regime, inverses)
    image = operate(precond, diagonal)
    inner_rz, inner_wz = paired(residual, precond, image)
    step_len = inner_rz / inner_wz
    search = precond
    along = image
    for iteration in range(ITERS):
        solution = solution + step_len * search
        residual = residual - step_len * along
        if iteration + 1 < ITERS:
            precond = precondition(residual, regime, inverses)
            image = operate(precond, diagonal)
            rz_next, inner_wz = paired(residual, precond, image)
            scaling = rz_next / inner_rz
            step_len = rz_next / (inner_wz - scaling * rz_next / step_len)
            search = precond + scaling * search
            along = image + scaling * along
            inner_rz = rz_next
    solution, residual = sent_together((solution, residual), GZ, 0, 1, 2)
    return (solution, residual)


def solution(mesh):
    split = Mesh(
        mesh.devices.reshape(mesh.shape["gx"], 4, 2, 2, 2), ("gx", "gy_0", "gy_1", "gz_0", "gz_1")
    )
    in_specs = (P(GZ, "gx", GY), P(GZ, "gx", GY), P("gx", GY), P())
    out_specs = (P(GZ, "gx", GY), P(GZ, "gx", GY))
    return jax.shard_map(
        per_device, mesh=split, in_specs=in_specs, out_specs=out_specs, check_vma=False
    )
```

profile of v0, /device:TPU:1, one launch (start us, length us, event | category | flops | bytes accessed | tf_op | source)
XLA Modules:
  0.0 441.7 jit_solution(1391907388788264232)
XLA Ops:
  14.6 19.8 %all-to-all-done = f32[16,256,128]{2,0,1:T(8,128)S(1)} async-done(((f32[16,256,128]{2,0,1:T(8,128)}), f32[16,256,128]{2,0,1:T(8,128)S(1)}, u32[]{:S(2)}, u32[]{:S(2)}) %all-to-all-start) | async-done | bytes 2097184 | tf_op jit(solution)/shard_map/all_to_all | solution.py:92
  34.4 5.5 %all-to-all-start.1 = ((f32[16,256,128]{2,0,1:T(8,128)}), f32[16,256,128]{2,0,1:T(8,128)}, u32[]{:S(2)}, u32[]{:S(2)}) async-start(f32[16,256,128]{2,0,1:T(8,128)} %copy.127), calls=%async_computation.1 | async-start | bytes 4194304 | tf_op jit(solution)/shard_map/all_to_all | solution.py:93
  99.9 5.4 %select_maximum_fusion.8 = f32[66,66,130]{2,1,0:T(8,128)S(1)} fusion(f32[64,66,1]{2,1,0:T(8,128)} %copy.136, f32[64,66,1]{2,1,0:T(8,128)} %copy.135, f32[64,1,128]{2,1,0:T(1,128)S(1)} %bitcast.246, f32[64,64,128]{2,1,0:T(8,128)S(1)} %bitcast.230, f32[64,1,128]{2,1,0:T(1,128)S(1)} %bitcast.249), kind=kLoop, calls=%fused_computation.55 | loop fusion | flops 6795360 | bytes 4461600 | tf_op jit(solution)/shard_map/concatenate | solution.py:21
  105.4 5.7 %multiply_reduce_fusion.4 = (f32[]{:T(128)}, f32[64,64,128]{2,1,0:T(8,128)}) fusion(f32[8,8,64,128]{3,2,1,0:T(8,128)S(1)} %copy.167, f32[64,1,128]{2,1,0:T(1,128)S(1)} %bitcast.247, f32[64,64,128]{2,1,0:T(8,128)S(1)} %bitcast.231, f32[64,1,128]{2,1,0:T(1,128)S(1)} %bitcast.250, f32[64,66,1]{2,1,0:T(8,128)S(1)} %copy-done.15, ...), kind=kLoop, calls=%fused_computation.144 | loop fusion | flops 8912895 | bytes 12682244 | tf_op jit(solution)/shard_map/reduce_sum | solution.py:86
  111.1 9.4 %all-reduce.8 = (f32[]{:T(128)}, f32[]{:T(128)}) all-reduce(f32[]{:T(128)} %fusion.38, f32[]{:T(128)} %get-tuple-element.38), channel_id=1, replica_groups=mesh['gx'=4,'gy_0'=4,'gy_1'=2,'gz_0'=2,'gz_1'=2] {'gx'}, use_global_device_ids=true, to_apply=%region_1.2 | all-reduce | flops 2 | bytes 16 | tf_op jit(solution)/shard_map/psum | solution.py:34
  120.4 12.2 %all-reduce.5 = (f32[]{:T(128)}, f32[]{:T(128)}) all-reduce(f32[]{:T(128)} %get-tuple-element.16, f32[]{:T(128)} %get-tuple-element.17), channel_id=1, replica_groups=mesh['gx'=4,'gy_0'=4,'gy_1'=2,'gz_0'=2,'gz_1'=2] {'gy_0'}, use_global_device_ids=true, to_apply=%region_2.3 | all-reduce | flops 2 | bytes 16 | tf_op jit(solution)/shard_map/psum | solution.py:34
  132.6 6.0 %all-reduce.17 = (f32[]{:T(128)}, f32[]{:T(128)}) all-reduce(f32[]{:T(128)} %get-tuple-element.10, f32[]{:T(128)} %get-tuple-element.11), channel_id=1, replica_groups=mesh['gx'=4,'gy_0'=4,'gy_1'=2,'gz_0'=2,'gz_1'=2] {'gy_1'}, use_global_device_ids=true, to_apply=%region_3.4 | all-reduce | flops 2 | bytes 16 | tf_op jit(solution)/shard_map/psum | solution.py:34
  143.0 11.2 %all-reduce.11 = (f32[]{:T(128)}, f32[]{:T(128)}) all-reduce(f32[]{:T(128)} %get-tuple-element.28, f32[]{:T(128)} %get-tuple-element.29), channel_id=1, replica_groups=mesh['gx'=4,'gy_0'=4,'gy_1'=2,'gz_0'=2,'gz_1'=2] {'gz_1'}, use_global_device_ids=true, to_apply=%region_5.6 | all-reduce | flops 2 | bytes 16 | tf_op jit(solution)/shard_map/psum | solution.py:34
  202.5 5.5 %collective-permute-start.6 = (f32[64,66,1]{1,0,2:T(8,128)S(1)}, f32[64,66,1]{1,0,2:T(8,128)S(1)}, u32[]{:S(2)}, u32[]{:S(2)}) collective-permute-start(f32[64,66,1]{1,0,2:T(8,128)S(1)} %copy.145), channel_id=1, source_target_pairs={{0,4},{4,8},{8,12},{12,16},{16,20},{20,24},{24,28},{1,5},{5,9},{9,... | collective-permute-start | bytes 50696 | tf_op jit(solution)/shard_map/ppermute | solution.py:23
  212.5 6.2 %select_maximum_fusion.4 = f32[66,66,130]{2,1,0:T(8,128)S(1)} fusion(f32[64,66,1]{2,1,0:T(8,128)} %copy.148, f32[64,66,1]{2,1,0:T(8,128)} %copy.147, f32[64,1,128]{2,1,0:T(1,128)S(1)} %bitcast.255, f32[64,64,128]{2,1,0:T(8,128)} %bitcast.234, f32[64,1,128]{2,1,0:T(1,128)S(1)} %bitcast.261), kind=kLoop, calls=%fused_computation.51 | loop fusion | flops 6795360 | bytes 4461600 | tf_op jit(solution)/shard_map/concatenate | solution.py:21
  218.8 6.0 %multiply_reduce_fusion.2 = (f32[]{:T(128)}, f32[]{:T(128)}, f32[64,64,128]{2,1,0:T(8,128)}) fusion(f32[8,8,64,128]{3,2,1,0:T(8,128)S(1)} %copy-done.4, f32[64,64,128]{2,1,0:T(8,128)S(1)} %bitcast_subtract_fusion, f32[64,1,128]{2,1,0:T(1,128)S(1)} %bitcast.256, f32[64,64,128]{2,1,0:T(8,128)S(1)} %bitcast.235, f32[64,1,128]{2,1,0:T(1,128)S(1)} %bitcast.262, ...), kind=kLoop, calls=%fused_computation.142 | loop fusion | flops 9961470 | bytes 14779400 | tf_op jit(solution)/shard_map/reduce_sum | solution.py:86
  224.8 7.0 %all-reduce.7 = (f32[]{:T(128)}, f32[]{:T(128)}) all-reduce(f32[]{:T(128)} %get-tuple-element.5, f32[]{:T(128)} %get-tuple-element.4), channel_id=1, replica_groups=mesh['gx'=4,'gy_0'=4,'gy_1'=2,'gz_0'=2,'gz_1'=2] {'gx'}, use_global_device_ids=true, to_apply=%region_13.14 | all-reduce | flops 2 | bytes 16 | tf_op jit(solution)/shard_map/psum | solution.py:34
  231.8 9.4 %all-reduce.4 = (f32[]{:T(128)}, f32[]{:T(128)}) all-reduce(f32[]{:T(128)} %get-tuple-element.14, f32[]{:T(128)} %get-tuple-element.15), channel_id=1, replica_groups=mesh['gx'=4,'gy_0'=4,'gy_1'=2,'gz_0'=2,'gz_1'=2] {'gy_0'}, use_global_device_ids=true, to_apply=%region_14.15 | all-reduce | flops 2 | bytes 16 | tf_op jit(solution)/shard_map/psum | solution.py:34
  241.1 6.0 %all-reduce.16 = (f32[]{:T(128)}, f32[]{:T(128)}) all-reduce(f32[]{:T(128)} %get-tuple-element.8, f32[]{:T(128)} %get-tuple-element.9), channel_id=1, replica_groups=mesh['gx'=4,'gy_0'=4,'gy_1'=2,'gz_0'=2,'gz_1'=2] {'gy_1'}, use_global_device_ids=true, to_apply=%region_15.16 | all-reduce | flops 2 | bytes 16 | tf_op jit(solution)/shard_map/psum | solution.py:34
  251.6 13.5 %all-reduce.10 = (f32[]{:T(128)}, f32[]{:T(128)}) all-reduce(f32[]{:T(128)} %get-tuple-element.26, f32[]{:T(128)} %get-tuple-element.27), channel_id=1, replica_groups=mesh['gx'=4,'gy_0'=4,'gy_1'=2,'gz_0'=2,'gz_1'=2] {'gz_1'}, use_global_device_ids=true, to_apply=%region_17.18 | all-reduce | flops 2 | bytes 16 | tf_op jit(solution)/shard_map/psum | solution.py:34
  317.4 5.5 %collective-permute-start.10 = (f32[64,66,1]{1,0,2:T(8,128)S(1)}, f32[64,66,1]{1,0,2:T(8,128)S(1)}, u32[]{:S(2)}, u32[]{:S(2)}) collective-permute-start(f32[64,66,1]{1,0,2:T(8,128)S(1)} %copy.157), channel_id=1, source_target_pairs={{0,4},{4,8},{8,12},{12,16},{16,20},{20,24},{24,28},{1,5},{5,9},{9,... | collective-permute-start | bytes 50696 | tf_op jit(solution)/shard_map/ppermute | solution.py:23
  327.5 6.4 %select_maximum_fusion = f32[66,66,130]{2,1,0:T(8,128)S(1)} fusion(f32[64,66,1]{2,1,0:T(8,128)} %copy.160, f32[64,66,1]{2,1,0:T(8,128)} %copy.159, f32[64,1,128]{2,1,0:T(1,128)S(1)} %bitcast.252, f32[64,64,128]{2,1,0:T(8,128)} %bitcast.238, f32[64,1,128]{2,1,0:T(1,128)S(1)} %bitcast.258), kind=kLoop, calls=%fused_computation.47 | loop fusion | flops 6795360 | bytes 4461600 | tf_op jit(solution)/shard_map/concatenate | solution.py:21
  333.9 6.0 %multiply_reduce_fusion = (f32[]{:T(128)}, f32[]{:T(128)}, f32[64,64,128]{2,1,0:T(8,128)}) fusion(f32[8,8,64,128]{3,2,1,0:T(8,128)S(1)} %copy-done.6, f32[64,64,128]{2,1,0:T(8,128)S(1)} %multiply_subtract_fusion.1, f32[64,1,128]{2,1,0:T(1,128)S(1)} %bitcast.253, f32[64,64,128]{2,1,0:T(8,128)S(1)} %bitcast.239, f32[64,1,128]{2,1,0:T(1,128)S(1)} %bitcast.259, ...), kind=kLoop, calls=%fused_computation.138 | loop fusion | flops 9961470 | bytes 14779400 | tf_op jit(solution)/shard_map/reduce_sum | solution.py:86
  339.9 6.6 %all-reduce.6 = (f32[]{:T(128)}, f32[]{:T(128)}) all-reduce(f32[]{:T(128)} %get-tuple-element.3, f32[]{:T(128)} %get-tuple-element.2), channel_id=1, replica_groups=mesh['gx'=4,'gy_0'=4,'gy_1'=2,'gz_0'=2,'gz_1'=2] {'gx'}, use_global_device_ids=true, to_apply=%region_25.26 | all-reduce | flops 2 | bytes 16 | tf_op jit(solution)/shard_map/psum | solution.py:34
  346.6 7.5 %all-reduce.3 = (f32[]{:T(128)}, f32[]{:T(128)}) all-reduce(f32[]{:T(128)} %get-tuple-element.12, f32[]{:T(128)} %get-tuple-element.13), channel_id=1, replica_groups=mesh['gx'=4,'gy_0'=4,'gy_1'=2,'gz_0'=2,'gz_1'=2] {'gy_0'}, use_global_device_ids=true, to_apply=%region_26.27 | all-reduce | flops 2 | bytes 16 | tf_op jit(solution)/shard_map/psum | solution.py:34
  354.1 5.9 %all-reduce.15 = (f32[]{:T(128)}, f32[]{:T(128)}) all-reduce(f32[]{:T(128)} %get-tuple-element.6, f32[]{:T(128)} %get-tuple-element.7), channel_id=1, replica_groups=mesh['gx'=4,'gy_0'=4,'gy_1'=2,'gz_0'=2,'gz_1'=2] {'gy_1'}, use_global_device_ids=true, to_apply=%region_27.28 | all-reduce | flops 2 | bytes 16 | tf_op jit(solution)/shard_map/psum | solution.py:34
  364.5 13.4 %all-reduce.9 = (f32[]{:T(128)}, f32[]{:T(128)}) all-reduce(f32[]{:T(128)} %get-tuple-element.24, f32[]{:T(128)} %get-tuple-element.25), channel_id=1, replica_groups=mesh['gx'=4,'gy_0'=4,'gy_1'=2,'gz_0'=2,'gz_1'=2] {'gz_1'}, use_global_device_ids=true, to_apply=%region_29.30 | all-reduce | flops 2 | bytes 16 | tf_op jit(solution)/shard_map/psum | solution.py:34
  381.6 6.5 %multiply_subtract_fusion = (f32[64,64,128]{2,1,0:T(8,128)S(1)}, f32[64,64,128]{2,1,0:T(8,128)S(1)}) fusion(f32[64,64,128]{2,1,0:T(8,128)S(1)} %multiply_subtract_fusion.1, f32[64,64,128]{2,1,0:T(8,128)} %get-tuple-element.36, f32[]{:T(128)S(6)} %div.25, f32[]{:T(128)S(6)} %div.27, f32[64,64,128]{2,1,0:T(8,128)} %get-tuple-element.37, ...), kind=kLoop, calls=%fused_computation.136 | loop fusion | flops 7864320 | bytes 18874388 | tf_op jit(solution)/shard_map/sub | solution.py:105
  388.5 50.0 %all_to_all.45 = f32[64,64,256]{2,1,0:T(8,128)S(1)} all-to-all(f32[64,64,256]{2,1,0:T(8,128)S(1)} %pad_maximum_fusion), channel_id=1, replica_groups=mesh['gx'=4,'gy_0'=4,'gy_1'=2,'gz_0'=2,'gz_1'=2] {'gz_0','gz_1'}, dimensions={0} | all-to-all | bytes 8388608 | tf_op jit(solution)/shard_map/all_to_all | solution.py:46
  (125 shorter events, 194.3 us)
Async XLA Ops:
  4.8 29.7 %all-to-all-start = ((f32[16,256,128]{2,0,1:T(8,128)}), f32[16,256,128]{2,0,1:T(8,128)S(1)}, u32[]{:S(2)}, u32[]{:S(2)}) async-start(f32[16,256,128]{2,0,1:T(8,128)} %copy.125), calls=%async_computation | async-start | bytes 4194304 | tf_op jit(solution)/shard_map/all_to_all | solution.py:92
  34.4 38.6 %all-to-all-start.1 = ((f32[16,256,128]{2,0,1:T(8,128)}), f32[16,256,128]{2,0,1:T(8,128)}, u32[]{:S(2)}, u32[]{:S(2)}) async-start(f32[16,256,128]{2,0,1:T(8,128)} %copy.127), calls=%async_computation.1 | async-start | bytes 4194304 | tf_op jit(solution)/shard_map/all_to_all | solution.py:93
  40.6 22.8 %copy-start.1 = (f32[16,4,64,128]{3,2,0,1:T(8,128)}, f32[16,4,64,128]{3,2,0,1:T(8,128)S(1)}, u32[]{:S(2)}) copy-start(f32[16,4,64,128]{3,2,0,1:T(8,128)S(1)} %copy.126) | copy-start | bytes 6291460
  67.4 37.9 %copy-start.2 = (f32[8,8,64,128]{3,2,1,0:T(8,128)}, f32[8,8,64,128]{3,2,1,0:T(8,128)S(1)}, u32[]{:S(2)}) copy-start(f32[8,8,64,128]{3,2,1,0:T(8,128)S(1)} %copy.167) | copy-start | bytes 6291460
  67.4 8.6 %collective-permute-start.1 = (f32[64,1,128]{2,0,1:T(8,128)S(1)}, f32[64,1,128]{2,0,1:T(8,128)S(1)}, u32[]{:S(2)}, u32[]{:S(2)}) collective-permute-start(f32[64,1,128]{2,0,1:T(8,128)S(1)} %bitcast.264), channel_id=1, source_target_pairs={{1,0},{2,1},{3,2},{32,3},{33,32},{34,33},{35,34},{64,35},{65,64},{... | collective-permute-start | bytes 98312 | tf_op jit(solution)/shard_map/ppermute | solution.py:25
  69.4 6.7 %collective-permute-start = (f32[64,1,128]{2,0,1:T(8,128)S(1)}, f32[64,1,128]{2,0,1:T(8,128)S(1)}, u32[]{:S(2)}, u32[]{:S(2)}) collective-permute-start(f32[64,1,128]{2,0,1:T(8,128)S(1)} %bitcast.263), channel_id=1, source_target_pairs={{0,1},{1,2},{2,3},{3,32},{32,33},{33,34},{34,35},{35,64},{64,65},{... | collective-permute-start | bytes 98312 | tf_op jit(solution)/shard_map/ppermute | solution.py:23
  84.2 13.4 %collective-permute-start.2 = (f32[64,66,1]{1,0,2:T(8,128)S(1)}, f32[64,66,1]{1,0,2:T(8,128)S(1)}, u32[]{:S(2)}, u32[]{:S(2)}) collective-permute-start(f32[64,66,1]{1,0,2:T(8,128)S(1)} %copy.133), channel_id=1, source_target_pairs={{0,4},{4,8},{8,12},{12,16},{16,20},{20,24},{24,28},{1,5},{5,9},{9,... | collective-permute-start | bytes 50696 | tf_op jit(solution)/shard_map/ppermute | solution.py:23
  89.0 6.4 %collective-permute-start.3 = (f32[64,66,1]{1,0,2:T(8,128)S(1)}, f32[64,66,1]{1,0,2:T(8,128)S(1)}, u32[]{:S(2)}, u32[]{:S(2)}) collective-permute-start(f32[64,66,1]{1,0,2:T(8,128)S(1)} %copy.134), channel_id=1, source_target_pairs={{4,0},{8,4},{12,8},{16,12},{20,16},{24,20},{28,24},{5,1},{9,5},{13... | collective-permute-start | bytes 50696 | tf_op jit(solution)/shard_map/ppermute | solution.py:25
  158.1 60.6 %copy-start = (f32[64,64,128]{2,1,0:T(8,128)}, f32[64,64,128]{2,1,0:T(8,128)S(1)}, u32[]{:S(2)}) copy-start(f32[64,64,128]{2,1,0:T(8,128)S(1)} %bitcast_subtract_fusion) | copy-start | bytes 6291460
  186.4 6.6 %copy-start.3 = (f32[8,8,64,128]{3,2,1,0:T(8,128)}, f32[8,8,64,128]{3,2,1,0:T(8,128)S(1)}, u32[]{:S(2)}) copy-start(f32[8,8,64,128]{3,2,1,0:T(8,128)S(1)} %copy.170) | copy-start | bytes 6291460
  186.5 5.6 %collective-permute-start.5 = (f32[64,1,128]{2,0,1:T(8,128)S(1)}, f32[64,1,128]{2,0,1:T(8,128)S(1)}, u32[]{:S(2)}, u32[]{:S(2)}) collective-permute-start(f32[64,1,128]{2,0,1:T(8,128)S(1)} %bitcast.267), channel_id=1, source_target_pairs={{1,0},{2,1},{3,2},{32,3},{33,32},{34,33},{35,34},{64,35},{65,64},{... | collective-permute-start | bytes 98312 | tf_op jit(solution)/shard_map/ppermute | solution.py:25
  188.8 4.3 collective-permute-start.4
  198.7 9.3 %collective-permute-start.7 = (f32[64,66,1]{1,0,2:T(8,128)S(1)}, f32[64,66,1]{1,0,2:T(8,128)S(1)}, u32[]{:S(2)}, u32[]{:S(2)}) collective-permute-start(f32[64,66,1]{1,0,2:T(8,128)S(1)} %copy.146), channel_id=1, source_target_pairs={{4,0},{8,4},{12,8},{16,12},{20,16},{24,20},{28,24},{5,1},{9,5},{13... | collective-permute-start | bytes 50696 | tf_op jit(solution)/shard_map/ppermute | solution.py:25
  202.5 7.8 %collective-permute-start.6 = (f32[64,66,1]{1,0,2:T(8,128)S(1)}, f32[64,66,1]{1,0,2:T(8,128)S(1)}, u32[]{:S(2)}, u32[]{:S(2)}) collective-permute-start(f32[64,66,1]{1,0,2:T(8,128)S(1)} %copy.145), channel_id=1, source_target_pairs={{0,4},{4,8},{8,12},{12,16},{16,20},{20,24},{24,28},{1,5},{5,9},{9,... | collective-permute-start | bytes 50696 | tf_op jit(solution)/shard_map/ppermute | solution.py:23
  212.5 6.2 %copy-start.14 = (f32[64,66,1]{2,1,0:T(8,128)S(1)}, f32[64,66,1]{2,1,0:T(8,128)}, u32[]{:S(2)}) copy-start(f32[64,66,1]{2,1,0:T(8,128)} %copy.147) | copy-start | bytes 50692
  301.4 6.7 %copy-start.5 = (f32[8,8,64,128]{3,2,1,0:T(8,128)}, f32[8,8,64,128]{3,2,1,0:T(8,128)S(1)}, u32[]{:S(2)}) copy-start(f32[8,8,64,128]{3,2,1,0:T(8,128)S(1)} %copy.172) | copy-start | bytes 6291460
  301.4 5.6 %collective-permute-start.9 = (f32[64,1,128]{2,0,1:T(8,128)S(1)}, f32[64,1,128]{2,0,1:T(8,128)S(1)}, u32[]{:S(2)}, u32[]{:S(2)}) collective-permute-start(f32[64,1,128]{2,0,1:T(8,128)S(1)} %bitcast.268), channel_id=1, source_target_pairs={{1,0},{2,1},{3,2},{32,3},{33,32},{34,33},{35,34},{64,35},{65,64},{... | collective-permute-start | bytes 98312 | tf_op jit(solution)/shard_map/ppermute | solution.py:25
  303.7 4.3 collective-permute-start.8
  313.7 9.3 %collective-permute-start.11 = (f32[64,66,1]{1,0,2:T(8,128)S(1)}, f32[64,66,1]{1,0,2:T(8,128)S(1)}, u32[]{:S(2)}, u32[]{:S(2)}) collective-permute-start(f32[64,66,1]{1,0,2:T(8,128)S(1)} %copy.158), channel_id=1, source_target_pairs={{4,0},{8,4},{12,8},{16,12},{20,16},{24,20},{28,24},{5,1},{9,5},{13... | collective-permute-start | bytes 50696 | tf_op jit(solution)/shard_map/ppermute | solution.py:25
  317.4 7.8 %collective-permute-start.10 = (f32[64,66,1]{1,0,2:T(8,128)S(1)}, f32[64,66,1]{1,0,2:T(8,128)S(1)}, u32[]{:S(2)}, u32[]{:S(2)}) collective-permute-start(f32[64,66,1]{1,0,2:T(8,128)S(1)} %copy.157), channel_id=1, source_target_pairs={{0,4},{4,8},{8,12},{12,16},{16,20},{20,24},{24,28},{1,5},{5,9},{9,... | collective-permute-start | bytes 50696 | tf_op jit(solution)/shard_map/ppermute | solution.py:23
  327.5 6.4 %copy-start.6 = (f32[8,8,64,128]{3,2,1,0:T(8,128)S(1)}, f32[8,8,64,128]{3,2,1,0:T(8,128)}, u32[]{:S(2)}) copy-start(f32[8,8,64,128]{3,2,1,0:T(8,128)} %copy-done.5) | copy-start | bytes 6291460
  327.5 6.4 %copy-start.9 = (f32[16,4,64,128]{3,2,0,1:T(8,128)S(1)}, f32[16,4,64,128]{3,2,0,1:T(8,128)}, u32[]{:S(2)}) copy-start(f32[16,4,64,128]{3,2,0,1:T(8,128)} %copy.128) | copy-start | bytes 6291460
  327.5 6.4 %copy-start.10 = (f32[64,66,1]{2,1,0:T(8,128)S(1)}, f32[64,66,1]{2,1,0:T(8,128)}, u32[]{:S(2)}) copy-start(f32[64,66,1]{2,1,0:T(8,128)} %copy.160) | copy-start | bytes 50692
  327.5 6.4 %copy-start.13 = (f32[64,66,1]{2,1,0:T(8,128)S(1)}, f32[64,66,1]{2,1,0:T(8,128)}, u32[]{:S(2)}) copy-start(f32[64,66,1]{2,1,0:T(8,128)} %copy.159) | copy-start | bytes 50692
  (9 other events, 44.7 us)
where the time goes:
time: 446 us; the launch traced here: 442 us
  blocking collectives  171 us (38%)
  matrix products  81.7 us (18%)
  other arithmetic  56.9 us (13%)
  local copies, waits for them, and re-layouts  52.2 us (12%)
  starting transfers between devices  46.9 us (11%)
  waiting for transfers between devices  21.8 us (5%)
  between operations  10.8 us (2%)
    psum x15, blocking collectives, over_axes(): x = lax.psum(x, axis)  121 us
    dot_general x24, matrix products, apply_blocks(): jnp.dot(matrices[member], flattened, precision=lax.Precision.HIGHEST)  81.7 us
    all_to_all x1, blocking collectives, sent_together(): lax.all_to_all(both, axis, split_axis=split_dim, concat_axis=concat_dim,...  50 us
    ppermute x6, starting transfers between devices, extended(): lax.ppermute(tail, axis, [(i, (i + 1) % count) for i in range(ends)])  26 us
    all_to_all x1, waiting for transfers between devices, per_device(): lax.all_to_all(right_side, GZ, split_axis=1, concat_axis=0, tiled=True)  19.8 us
    concatenate x6, other arithmetic, extended(): jnp.concatenate([lax.ppermute(tail, axis, [(i, (i + 1) % count) for i in...  19.1 us
    reduce_sum x3, other arithmetic, paired(): jnp.sum(image * precond)  17.7 us
    slice x6, local copies, waits for them, and re-layouts, extended(): head = lax.slice_in_dim(cells, 0, width, axis=dim)  15.9 us
  transfers between devices with their start and end apart: 14, of which 3 were waited for; matrix products, arithmetic and copies ran while one was open for 12% of the time, Pallas kernels for 0%

commit v1 on v0

v1 whole, which is shorter than its diff:
```python
import functools

import jax
import jax.numpy as jnp
from jax import lax
from jax.experimental import pallas as pl
from jax.experimental.pallas import tpu as pltpu
from jax.sharding import PartitionSpec as P

f32 = jnp.float32
bf16 = jnp.bfloat16
MESH = pl.DeviceIdType.MESH
NREG = 8
ROWS = 64
DEEP = 64
SLAB = 16
LANES = 128
CHUNK = 16
STEPS = ROWS // CHUNK


def halves(v):
    high = v.astype(bf16)
    return high, (v - high.astype(f32)).astype(bf16)


def tiled(v):
    return v.reshape(DEEP // 8, 8, LANES)


def flat(v):
    return v.reshape(DEEP, LANES)


def kernel(
    right_side, diagonal, regime, blocks,
    out_sol, out_res,
    res, diag, u0, m0, m1, w0, n0, u1, w1, p1, x2, s1, fin, finr,
    reg, inv, stack, edge, left, right, sum_a, sum_b, sum_c,
    col_sem, in_send, small_sem, halo_recv, halo_send, sum_recv, sum_send, out_recv, out_send,
):
    gx, gy, gz = lax.axis_index("gx"), lax.axis_index("gy"), lax.axis_index("gz")
    odd = lax.rem(gx, 2)
    part = gz + odd * (3 - 2 * gz)
    stride = 1 - 2 * odd
    first, last = (3 - part) // 3, part // 3
    line = gx * 4 + part
    lower = {"gx": gx - first, "gz": gz - stride * (1 - first)}
    upper = {"gx": gx + last, "gz": gz + stride * (1 - last)}
    has_lower, has_upper = line > 0, line < 15
    has_left, has_right = gy > 0, gy < 7

    def others(axis, me, count):
        return [{axis: lax.rem(me + j, count)} for j in range(1, count)]

    barrier = pltpu.get_barrier_semaphore()
    peers = others("gz", gz, 4) + others("gx", gx, 4) + others("gy", gy, 8)
    for peer in peers:
        pl.semaphore_signal(barrier, inc=1, device_id=peer, device_id_type=MESH)

    small = [
        pltpu.make_async_copy(blocks, inv, small_sem.at[0]),
        pltpu.make_async_copy(
            regime.at[pl.ds(pl.multiple_of(part * ROWS, ROWS), ROWS), :], reg, small_sem.at[1]
        ),
    ]
    for copy in small:
        copy.start()
    base = pl.multiple_of(gz * SLAB, SLAB)

    def part_of(k):
        return k + odd * (3 - 2 * k)

    def send_columns(array, source, target, c):
        def body(d, carry):
            rows = pl.ds(c * CHUNK, CHUNK)
            for j in range(1, 4):
                k = lax.rem(gz + j, 4)
                begin = pl.multiple_of(part_of(k) * ROWS + c * CHUNK, CHUNK)
                pltpu.make_async_remote_copy(
                    source.at[d, pl.ds(begin, CHUNK), :],
                    target.at[rows, base + d, :],
                    in_send.at[array],
                    col_sem.at[array, c],
                    device_id={"gz": k},
                    device_id_type=MESH,
                ).start()
            begin = pl.multiple_of(part * ROWS + c * CHUNK, CHUNK)
            pltpu.make_async_copy(
                source.at[d, pl.ds(begin, CHUNK), :],
                target.at[rows, base + d, :],
                col_sem.at[array, c],
            ).start()
            return carry

        lax.fori_loop(0, SLAB, body, 0)

    pl.semaphore_wait(barrier, 13)
    for c in range(STEPS):
        send_columns(0, right_side, res, c)
    for c in range(STEPS // 2):
        send_columns(1, diagonal, diag, c)

    nothing = jnp.zeros((DEEP, LANES), f32)
    for array in (u0, m0, m1):

        @pl.when(line == 0)
        def _():
            array[0] = nothing

        @pl.when(line == 15)
        def _():
            array[ROWS + 1] = nothing

    for it in range(3):

        @pl.when(gy == 0)
        def _():
            left[it] = nothing

        @pl.when(gy == 7)
        def _():
            right[it] = nothing

        edge[it, 0] = nothing
        edge[it, 1] = nothing

    for copy in small:
        copy.wait()
    high, low = halves(inv[...])
    stack[...] = jnp.concatenate([high, high, low, low], axis=1)

    lane = lax.broadcasted_iota(jnp.int32, (DEEP, LANES), 1)

    def apply_blocks(source, target, it, c):
        to_left, to_right = edge[it, 0], edge[it, 1]
        for h in range(CHUNK // 2):
            x = c * CHUNK + 2 * h
            both = jnp.concatenate([source[x], source[x + 1]], axis=1)
            high, low = halves(both)
            out = jnp.dot(
                stack[...],
                jnp.concatenate([high, low, high, low], axis=0),
                preferred_element_type=f32,
            )
            kind = jnp.concatenate([reg[pl.ds(x, 1), :], reg[pl.ds(x + 1, 1), :]], axis=1)
            kind = jnp.broadcast_to(kind, (DEEP, 2 * LANES))
            some = [out[k * DEEP : (k + 1) * DEEP] for k in range(NREG)]
            for bit in range(3):
                chosen = (kind & (1 << bit)) != 0
                some = [jnp.where(chosen, some[i + 1], some[i]) for i in range(0, len(some), 2)]
            for j in range(2):
                z = some[0][:, j * LANES : (j + 1) * LANES]
                target[x + j + 1] = z
                here = lane == x + j
                to_left = jnp.where(here, pltpu.roll(z, x + j, 1), to_left)
                to_right = jnp.where(here, pltpu.roll(z, x + j + 1, 1), to_right)
        edge[it, 0] = to_left
        edge[it, 1] = to_right

    def halo_copies(array, it):
        def copy(k, source, target, device):
            return pltpu.make_async_remote_copy(
                source, target, halo_send.at[it, k], halo_recv.at[it, k],
                device_id=device, device_id_type=MESH,
            )

        return (
            (has_lower, has_upper, copy(0, array.at[1], array.at[ROWS + 1], lower)),
            (has_upper, has_lower, copy(1, array.at[ROWS], array.at[0], upper)),
            (has_left, has_right, copy(2, edge.at[it, 0], right.at[it], {"gy": gy - 1})),
            (has_right, has_left, copy(3, edge.at[it, 1], left.at[it], {"gy": gy + 1})),
        )

    def start_halo(array, it):
        for sends, _, copy in halo_copies(array, it):
            pl.when(sends)(copy.start)

    def wait_halo(array, it):
        for _, receives, copy in halo_copies(array, it):
            pl.when(receives)(copy.wait_recv)

    def stencil(array, it, x):
        v = array[x + 1]
        beside = array[x] + array[x + 2]
        empty = jnp.zeros((1, LANES), f32)
        beside = beside + jnp.concatenate([empty, v[:-1]], axis=0)
        beside = beside + jnp.concatenate([v[1:], empty], axis=0)
        from_left = pltpu.roll(left[it], lax.rem(LANES - x, LANES), 1)
        from_right = pltpu.roll(right[it], LANES - 1 - x, 1)
        beside = beside + jnp.where(lane == 0, from_left, pltpu.roll(v, 1, 1))
        beside = beside + jnp.where(lane == LANES - 1, from_right, pltpu.roll(v, LANES - 1, 1))
        return v, (6.0 + diag[x]) * v - beside

    sums = ((sum_a, "gz", gz, 4), (sum_b, "gx", gx, 4), (sum_c, "gy", gy, 8))

    def start_sum(it, stage, value):
        buffer, axis, me, count = sums[stage]
        buffer[it, me] = value
        for peer in others(axis, me, count):
            pltpu.make_async_remote_copy(
                buffer.at[it, me], buffer.at[it, me], sum_send.at[it, stage], sum_recv.at[it, stage],
                device_id=peer, device_id_type=MESH,
            ).start()

    def end_sum(it, stage):
        buffer, _, _, count = sums[stage]
        some = buffer.at[it, pl.ds(0, count - 1)]
        pltpu.make_async_copy(some, some, sum_recv.at[it, stage]).wait()
        total = buffer[it, 0]
        for k in range(1, count):
            total = total + buffer[it, k]
        return total

    def totals(it):
        total = end_sum(it, 2)
        whole = [jnp.sum(total[k], keepdims=True) for k in range(2)]
        return [jnp.broadcast_to(t, (8, LANES)) for t in whole]

    def folded(v):
        return jnp.sum(tiled(v), axis=0)

    def rows_of(c, body, carry):
        return lax.fori_loop(c * CHUNK, (c + 1) * CHUNK, body, carry)

    zero = jnp.zeros((8, LANES), f32)

    def first_precond(c, carry):
        some = res.at[pl.ds(pl.multiple_of(c * CHUNK, CHUNK), CHUNK)]
        pltpu.make_async_copy(some, some, col_sem.at[0, c]).wait()
        apply_blocks(res, u0, 0, c)
        return carry

    lax.fori_loop(0, STEPS, first_precond, 0)
    start_halo(u0, 0)
    for c in range(STEPS // 2, STEPS):
        send_columns(1, diagonal, diag, c)
    wait_halo(u0, 0)

    def first_image(c, carry):
        some = diag.at[pl.ds(pl.multiple_of(c * CHUNK, CHUNK), CHUNK)]
        pltpu.make_async_copy(some, some, col_sem.at[1, c]).wait()

        def body(x, carry):
            rz, wz = carry
            u, w = stencil(u0, 0, x)
            w0[x] = w
            return rz + folded(res[x] * u), wz + folded(w * u)

        return rows_of(c, body, carry)

    rz, wz = lax.fori_loop(0, STEPS, first_image, (zero, zero))

    def blocks_beside_sum(it, source, target):
        def body(c, carry):
            apply_blocks(source, target, it + 1, c)
            for stage in range(2):

                @pl.when(c == 2 * stage)
                def _():
                    start_sum(it, stage + 1, end_sum(it, stage))

            return carry

        lax.fori_loop(0, STEPS, body, 0)

    start_sum(0, 0, jnp.stack([rz, wz]))
    blocks_beside_sum(0, w0, m0)
    start_halo(m0, 1)
    rz0, wz0 = totals(0)
    alpha0 = rz0 / wz0
    wait_halo(m0, 1)

    def second(x, carry):
        rz, wz = carry
        m, n = stencil(m0, 1, x)
        n0[x] = n
        w = w0[x]
        r = flat(tiled(res[x]) - alpha0 * tiled(w))
        u = flat(tiled(u0[x + 1]) - alpha0 * tiled(m))
        w = flat(tiled(w) - alpha0 * tiled(n))
        res[x] = r
        u1[x] = u
        w1[x] = w
        return rz + folded(r * u), wz + folded(w * u)

    rz, wz = lax.fori_loop(0, ROWS, second, (zero, zero))
    start_sum(1, 0, jnp.stack([rz, wz]))
    blocks_beside_sum(1, w1, m1)
    start_halo(m1, 2)
    rz1, wz1 = totals(1)
    beta1 = rz1 / rz0
    alpha1 = rz1 / (wz1 - beta1 * rz1 / alpha0)
    wait_halo(m1, 2)

    def third(x, carry):
        rz, wz = carry
        m, n = stencil(m1, 2, x)
        first_u, first_w = tiled(u0[x + 1]), tiled(w0[x])
        u, w = tiled(u1[x]), tiled(w1[x])
        p = u + beta1 * first_u
        s = w + beta1 * first_w
        r = tiled(res[x]) - alpha1 * s
        u = u - alpha1 * (tiled(m) + beta1 * tiled(m0[x + 1]))
        w = w - alpha1 * (tiled(n) + beta1 * tiled(n0[x]))
        p1[x] = flat(p)
        s1[x] = flat(s)
        x2[x] = flat(alpha0 * first_u + alpha1 * p)
        res[x] = flat(r)
        u1[x] = flat(u)
        w1[x] = flat(w)
        return rz + folded(flat(r * u)), wz + folded(flat(w * u))

    rz, wz = lax.fori_loop(0, ROWS, third, (zero, zero))
    start_sum(2, 0, jnp.stack([rz, wz]))
    start_sum(2, 1, end_sum(2, 0))
    start_sum(2, 2, end_sum(2, 1))
    rz2, wz2 = totals(2)
    beta2 = rz2 / rz1
    alpha2 = rz2 / (wz2 - beta2 * rz2 / alpha1)

    def last_rows(x, carry):
        p = tiled(u1[x]) + beta2 * tiled(p1[x])
        s = tiled(w1[x]) + beta2 * tiled(s1[x])
        fin[x] = flat(tiled(x2[x]) + alpha2 * p)
        finr[x] = flat(tiled(res[x]) - alpha2 * s)
        return carry

    lax.fori_loop(0, ROWS, last_rows, 0)

    mine = pl.ds(pl.multiple_of(part * ROWS, ROWS), ROWS)
    for array, (source, target) in enumerate(((fin, out_sol), (finr, out_res))):

        def send_back(d, carry):
            for j in range(1, 4):
                k = lax.rem(gz + j, 4)
                pltpu.make_async_remote_copy(
                    source.at[:, k * SLAB + d, :],
                    target.at[d, mine, :],
                    out_send.at[array],
                    out_recv.at[array],
                    device_id={"gz": k},
                    device_id_type=MESH,
                ).start()
            pltpu.make_async_copy(
                source.at[:, base + d, :], target.at[d, mine, :], out_recv.at[array]
            ).start()
            return carry

        lax.fori_loop(0, SLAB, send_back, 0)

    for array, target in enumerate((out_sol, out_res)):
        pltpu.make_async_copy(target, target, out_recv.at[array]).wait()
    for array in range(2):
        some = res.at[pl.ds(0, 3 * SLAB)]
        pltpu.make_async_copy(some, some, in_send.at[array]).wait()
        pltpu.make_async_copy(some, some, out_send.at[array]).wait()
    for it, array in enumerate((u0, m0, m1)):
        for sends, _, copy in halo_copies(array, it):
            pl.when(sends)(copy.wait_send)
        for stage, (buffer, _, _, count) in enumerate(sums):
            some = buffer.at[it, pl.ds(0, count - 1)]
            pltpu.make_async_copy(some, some, sum_send.at[it, stage]).wait()


def per_device(right_side, diagonal, regime, inverses):
    shape = jax.ShapeDtypeStruct(right_side.shape, f32)
    field = pltpu.VMEM((ROWS, DEEP, LANES), f32)
    padded = pltpu.VMEM((ROWS + 2, DEEP, LANES), f32)
    plane = (DEEP, LANES)
    return pl.pallas_call(
        kernel,
        out_shape=(shape, shape),
        in_specs=[pl.BlockSpec(memory_space=pl.ANY)] * 4,
        out_specs=[pl.BlockSpec(memory_space=pl.ANY)] * 2,
        scratch_shapes=[field, field, padded, padded, padded] + [field] * 9 + [
            pltpu.VMEM((ROWS, LANES), jnp.int32),
            pltpu.VMEM((NREG * DEEP, DEEP), f32),
            pltpu.VMEM((NREG * DEEP, 4 * DEEP), bf16),
            pltpu.VMEM((3, 2) + plane, f32),
            pltpu.VMEM((3,) + plane, f32),
            pltpu.VMEM((3,) + plane, f32),
            pltpu.VMEM((3, 4, 2, 8, LANES), f32),
            pltpu.VMEM((3, 4, 2, 8, LANES), f32),
            pltpu.VMEM((3, 8, 2, 8, LANES), f32),
            pltpu.SemaphoreType.DMA((2, STEPS)),
            pltpu.SemaphoreType.DMA((2,)),
            pltpu.SemaphoreType.DMA((2,)),
            pltpu.SemaphoreType.DMA((3, 4)),
            pltpu.SemaphoreType.DMA((3, 4)),
            pltpu.SemaphoreType.DMA((3, 3)),
            pltpu.SemaphoreType.DMA((3, 3)),
            pltpu.SemaphoreType.DMA((2,)),
            pltpu.SemaphoreType.DMA((2,)),
        ],
        compiler_params=pltpu.CompilerParams(
            collective_id=0, has_side_effects=True, vmem_limit_bytes=60 * 2**20
        ),
    )(right_side, diagonal, regime, inverses.reshape(NREG * DEEP, DEEP))


def solution(mesh):
    field = P("gz", "gx", "gy")
    return jax.shard_map(
        per_device,
        mesh=mesh,
        in_specs=(field, field, P("gx", "gy"), P()),
        out_specs=(field, field),
        check_vma=False,
    )
```

time: 446 us -> 158 us (0.35)
  blocking collectives: 171 us -> 0 us
  Pallas kernels: 0 us -> 153 us
  matrix products: 81.7 us -> 0 us
  other arithmetic: 56.9 us -> 0 us
  local copies, waits for them, and re-layouts: 52.2 us -> 4.58 us
  starting transfers between devices: 46.9 us -> 0 us
  waiting for transfers between devices: 21.8 us -> 0 us
  between operations: 10.8 us -> 0.65 us
    pallas_call x0 -> x1, Pallas kernels: none -> 153 us  [per_device(): pl.pallas_call(kernel, out_shape=(shape, shape), in_specs=[pl.BlockSpec(m...]
    psum x15 -> x0, blocking collectives: 121 us -> none  [over_axes(): x = lax.psum(x, axis)]
    dot_general x24 -> x0, matrix products: 81.7 us -> none  [apply_blocks(): jnp.dot(matrices[member], flattened, precision=lax.Precision.HIGHEST)]
    all_to_all x1 -> x0, blocking collectives: 50 us -> none  [sent_together(): lax.all_to_all(both, axis, split_axis=split_dim, concat_axis=concat_dim,...]
    ppermute x12 -> x0, starting transfers between devices: 36.4 us -> none  [the longest x6 26 us: extended(): lax.ppermute(tail, axis, [(i, (i + 1) % count) for i in range(ends)])]
    slice x12 -> x0, local copies, waits for them, and re-layouts: 23.4 us -> none  [the longest x6 15.9 us: extended(): head = lax.slice_in_dim(cells, 0, width, axis=dim)]
    reduce_sum x4 -> x0, other arithmetic: 20.8 us -> none  [the longest x3 17.7 us: paired(): jnp.sum(image * precond)]
    all_to_all x2 -> x0, waiting for transfers between devices: 19.8 us -> none  [the longest x1 19.8 us: per_device(): lax.all_to_all(right_side, GZ, split_axis=1, concat_axis=0, tiled=True)]
  transfers between devices with their start and end apart: 14 -> 0, of which waited for: 3 -> 0; matrix products, arithmetic and copies ran while one was open for 12% -> 0% of each run, Pallas kernels for 0% -> 0%
where the time goes in v1:
time: 158 us
  Pallas kernels  153 us (97%)
  local copies, waits for them, and re-layouts  4.58 us (3%)
    pallas_call x1, Pallas kernels, per_device(): pl.pallas_call(kernel, out_shape=(shape, shape), in_specs=[pl.BlockSpec(m...  153 us
    unnamed x4, local copies, waits for them, and re-layouts  4.58 us

profile of v1, /device:TPU:1, one launch (start us, length us, event | category | flops | bytes accessed | tf_op | source)
XLA Modules:
  0.0 158.2 jit_solution(12683479799102468831)
XLA Ops:
  0.6 152.9 %shard_map.59 = (f32[16,256,128]{2,1,0:T(8,128)}, f32[16,256,128]{2,1,0:T(8,128)}) custom-call(f32[16,256,128]{2,1,0:T(8,128)} %right_side.1, f32[16,256,128]{2,1,0:T(8,128)} %diagonal.1, s32[256,128]{1,0:T(8,128)} %regime.1, f32[512,64]{1,0:T(8,128)} %bitcast.1), custom_call_target="tpu_custom_call" | custom-call | tf_op jit(solution)/shard_map/pallas_call | solution.py:371
  153.6 0.0 copy-start
  153.6 3.3 %copy.8 = f32[16,256,128]{2,1,0:T(8,128)} copy(f32[16,256,128]{2,1,0:T(8,128)} %get-tuple-element.4) | data formatting | bytes 4194304
  156.8 0.0 copy-done
  156.8 1.3 copy.9
Async XLA Ops:
  153.6 3.3 %copy-start = (f32[16,256,128]{2,1,0:T(8,128)S(1)}, f32[16,256,128]{2,1,0:T(8,128)}, u32[]{:S(2)}) copy-start(f32[16,256,128]{2,1,0:T(8,128)} %get-tuple-element.5) | copy-start | bytes 6291460

commit v2 on v1

--- a/solution.py
+++ b/solution.py
@@ -17,6 +17,8 @@
 LANES = 128
 CHUNK = 16
 STEPS = ROWS // CHUNK
+UNROLL = 8
+GROUP = 4
 
 
 def halves(v):
@@ -34,10 +36,10 @@
 
 def kernel(
     right_side, diagonal, regime, blocks,
-    out_sol, out_res,
-    res, diag, u0, m0, m1, w0, n0, u1, w1, p1, x2, s1, fin, finr,
-    reg, inv, stack, edge, left, right, sum_a, sum_b, sum_c,
-    col_sem, in_send, small_sem, halo_recv, halo_send, sum_recv, sum_send, out_recv, out_send,
+    out_sol, out_sides, out_ends,
+    res, diag, u0, m0, m1, w0, n0, w1, fin,
+    reg, inv, stack, edge, left, right, sides, blank, sum_a, sum_b, sum_c,
+    col_sem, in_send, small_sem, halo_recv, halo_send, sum_recv, sum_send, out_recv, sides_recv, ends_recv, out_send,
 ):
     gx, gy, gz = lax.axis_index("gx"), lax.axis_index("gy"), lax.axis_index("gz")
     odd = lax.rem(gx, 2)
@@ -102,6 +104,7 @@
         send_columns(1, diagonal, diag, c)
 
     nothing = jnp.zeros((DEEP, LANES), f32)
+    blank[...] = nothing
     for array in (u0, m0, m1):
 
         @pl.when(line == 0)
@@ -220,8 +223,17 @@
     def folded(v):
         return jnp.sum(tiled(v), axis=0)
 
+    def many(body):
+        def some(i, carry):
+            for j in range(UNROLL):
+                carry = body(i * UNROLL + j, carry)
+            return carry
+
+        return some
+
     def rows_of(c, body, carry):
-        return lax.fori_loop(c * CHUNK, (c + 1) * CHUNK, body, carry)
+        begin = c * (CHUNK // UNROLL)
+        return lax.fori_loop(begin, begin + CHUNK // UNROLL, many(body), carry)
 
     zero = jnp.zeros((8, LANES), f32)
 
@@ -275,16 +287,14 @@
         rz, wz = carry
         m, n = stencil(m0, 1, x)
         n0[x] = n
-        w = w0[x]
-        r = flat(tiled(res[x]) - alpha0 * tiled(w))
-        u = flat(tiled(u0[x + 1]) - alpha0 * tiled(m))
-        w = flat(tiled(w) - alpha0 * tiled(n))
-        res[x] = r
-        u1[x] = u
-        w1[x] = w
-        return rz + folded(r * u), wz + folded(w * u)
-
-    rz, wz = lax.fori_loop(0, ROWS, second, (zero, zero))
+        w = tiled(w0[x])
+        r = tiled(res[x]) - alpha0 * w
+        u = tiled(u0[x + 1]) - alpha0 * tiled(m)
+        w = w - alpha0 * tiled(n)
+        w1[x] = flat(w)
+        return rz + jnp.sum(r * u, axis=0), wz + jnp.sum(w * u, axis=0)
+
+    rz, wz = lax.fori_loop(0, ROWS // UNROLL, many(second), (zero, zero))
     start_sum(1, 0, jnp.stack([rz, wz]))
     blocks_beside_sum(1, w1, m1)
     start_halo(m1, 2)
@@ -296,22 +306,14 @@
     def third(x, carry):
         rz, wz = carry
         m, n = stencil(m1, 2, x)
-        first_u, first_w = tiled(u0[x + 1]), tiled(w0[x])
-        u, w = tiled(u1[x]), tiled(w1[x])
-        p = u + beta1 * first_u
-        s = w + beta1 * first_w
-        r = tiled(res[x]) - alpha1 * s
-        u = u - alpha1 * (tiled(m) + beta1 * tiled(m0[x + 1]))
-        w = w - alpha1 * (tiled(n) + beta1 * tiled(n0[x]))
-        p1[x] = flat(p)
-        s1[x] = flat(s)
-        x2[x] = flat(alpha0 * first_u + alpha1 * p)
-        res[x] = flat(r)
-        u1[x] = flat(u)
-        w1[x] = flat(w)
-        return rz + folded(flat(r * u)), wz + folded(flat(w * u))
-
-    rz, wz = lax.fori_loop(0, ROWS, third, (zero, zero))
+        first_w, second_w = tiled(w0[x]), tiled(w1[x])
+        r = tiled(res[x]) - alpha0 * first_w - alpha1 * (second_w + beta1 * first_w)
+        second_m = tiled(m0[x + 1])
+        u = tiled(u0[x + 1]) - alpha0 * second_m - alpha1 * (tiled(m) + beta1 * second_m)
+        w = second_w - alpha1 * (tiled(n) + beta1 * tiled(n0[x]))
+        return rz + jnp.sum(r * u, axis=0), wz + jnp.sum(w * u, axis=0)
+
+    rz, wz = lax.fori_loop(0, ROWS // UNROLL, many(third), (zero, zero))
     start_sum(2, 0, jnp.stack([rz, wz]))
     start_sum(2, 1, end_sum(2, 0))
     start_sum(2, 2, end_sum(2, 1))
@@ -319,48 +321,168 @@
     beta2 = rz2 / rz1
     alpha2 = rz2 / (wz2 - beta2 * rz2 / alpha1)
 
+    by_u = alpha0 + alpha1 * (1.0 + beta1) + alpha2 * (1.0 + beta2 * (1.0 + beta1))
+    by_m = -alpha1 * alpha0 - alpha2 * (alpha0 + alpha1 * beta1 + beta2 * alpha0)
+    by_n = -alpha2 * alpha1
+
+    def joined(u, m, n):
+        return flat(by_u * tiled(u) + by_m * tiled(m) + by_n * tiled(n))
+
     def last_rows(x, carry):
-        p = tiled(u1[x]) + beta2 * tiled(p1[x])
-        s = tiled(w1[x]) + beta2 * tiled(s1[x])
-        fin[x] = flat(tiled(x2[x]) + alpha2 * p)
-        finr[x] = flat(tiled(res[x]) - alpha2 * s)
+        fin[x] = joined(u0[x], m0[x], m1[x])
         return carry
 
-    lax.fori_loop(0, ROWS, last_rows, 0)
+    lax.fori_loop(0, (ROWS + 2) // 6, lambda i, k: [last_rows(6 * i + j, k) for j in range(6)][0], 0)
+    from_left, from_right = joined(left[0], left[1], left[2]), joined(right[0], right[1], right[2])
+    sides[...] = jnp.where(lane < ROWS, from_left, pltpu.roll(from_right, ROWS, 1))
 
     mine = pl.ds(pl.multiple_of(part * ROWS, ROWS), ROWS)
-    for array, (source, target) in enumerate(((fin, out_sol), (finr, out_res))):
-
-        def send_back(d, carry):
-            for j in range(1, 4):
-                k = lax.rem(gz + j, 4)
-                pltpu.make_async_remote_copy(
-                    source.at[:, k * SLAB + d, :],
-                    target.at[d, mine, :],
-                    out_send.at[array],
-                    out_recv.at[array],
-                    device_id={"gz": k},
-                    device_id_type=MESH,
-                ).start()
-            pltpu.make_async_copy(
-                source.at[:, base + d, :], target.at[d, mine, :], out_recv.at[array]
-            ).start()
-            return carry
-
-        lax.fori_loop(0, SLAB, send_back, 0)
-
-    for array, target in enumerate((out_sol, out_res)):
-        pltpu.make_async_copy(target, target, out_recv.at[array]).wait()
+    inner = fin.at[pl.ds(1, ROWS)]
+
+    def give(k, source, target, recv):
+        pltpu.make_async_remote_copy(
+            source, target, out_send, recv, device_id={"gz": k}, device_id_type=MESH
+        ).start()
+
+    def keep(source, target, recv):
+        pltpu.make_async_copy(source, target, recv).start()
+
+    for j in range(1, 4):
+        k = lax.rem(gz + j, 4)
+        near = pl.ds(pl.multiple_of(k * SLAB, SLAB), SLAB)
+        give(k, sides.at[near], out_sides.at[part], sides_recv)
+        for end, here in enumerate((part == 0, part == 3)):
+            row = end * (ROWS + 1)
+            pl.when(here)(functools.partial(give, k, fin.at[row, near], out_ends.at[end], ends_recv))
+
+        @pl.when(k > 0)
+        def _():
+            give(k, inner.at[:, k * SLAB - 1, :], out_sol.at[0, mine, :], out_recv)
+
+        @pl.when(k < 3)
+        def _():
+            give(k, inner.at[:, k * SLAB + SLAB, :], out_sol.at[SLAB + 1, mine, :], out_recv)
+
+    def send_back(d, carry):
+        for j in range(1, 4):
+            k = lax.rem(gz + j, 4)
+            give(k, inner.at[:, k * SLAB + d, :], out_sol.at[d + 1, mine, :], out_recv)
+        return carry
+
+    lax.fori_loop(0, SLAB, send_back, 0)
+
+    near = pl.ds(base, SLAB)
+    keep(sides.at[near], out_sides.at[part], sides_recv)
+    for end, here in enumerate((part == 0, part == 3)):
+        row = end * (ROWS + 1)
+        pl.when(here)(functools.partial(keep, fin.at[row, near], out_ends.at[end], ends_recv))
+
+    def keep_own(d, carry):
+        keep(inner.at[:, base + d, :], out_sol.at[d + 1, mine, :], out_recv)
+        return carry
+
+    lax.fori_loop(0, SLAB, keep_own, 0)
+    for outside, plane, depth in ((gz == 0, 0, base - 1), (gz == 3, SLAB + 1, base + SLAB)):
+
+        @pl.when(jnp.logical_not(outside))
+        def _():
+            keep(inner.at[:, depth, :], out_sol.at[plane, mine, :], out_recv)
+
+        @pl.when(outside)
+        def _():
+            for k in range(4):
+                keep(blank, out_sol.at[plane, pl.ds(k * ROWS, ROWS), :], out_recv)
+
+    some = res.at[pl.ds(0, 3 * SLAB)]
     for array in range(2):
-        some = res.at[pl.ds(0, 3 * SLAB)]
         pltpu.make_async_copy(some, some, in_send.at[array]).wait()
-        pltpu.make_async_copy(some, some, out_send.at[array]).wait()
     for it, array in enumerate((u0, m0, m1)):
         for sends, _, copy in halo_copies(array, it):
             pl.when(sends)(copy.wait_send)
         for stage, (buffer, _, _, count) in enumerate(sums):
-            some = buffer.at[it, pl.ds(0, count - 1)]
-            pltpu.make_async_copy(some, some, sum_send.at[it, stage]).wait()
+            group = buffer.at[it, pl.ds(0, count - 1)]
+            pltpu.make_async_copy(group, group, sum_send.at[it, stage]).wait()
+    for target, recv in ((out_sides, sides_recv), (out_ends, ends_recv), (out_sol, out_recv)):
+        pltpu.make_async_copy(target, target, recv).wait()
+    pltpu.make_async_copy(some, some, out_send).wait()
+    pltpu.make_async_copy(sides.at[pl.ds(0, 3 * SLAB)], sides.at[pl.ds(0, 3 * SLAB)], out_send).wait()
+    for _ in range(4):
+        pltpu.make_async_copy(blank, blank, out_send).wait()
+
+    @pl.when(jnp.logical_or(gz == 0, gz == 3))
+    def _():
+        pltpu.make_async_copy(blank, blank, out_send).wait()
+
+    @pl.when(jnp.logical_or(part == 0, part == 3))
+    def _():
+        some_rows = blank.at[pl.ds(0, 3 * SLAB)]
+        pltpu.make_async_copy(some_rows, some_rows, out_send).wait()
+
+
+def residual_kernel(
+    right_side, diagonal, inner, sides, ends, out_sol, out_res,
+    sol, rhs, diag, res, side, end, turned, load, store,
+):
+    groups = SLAB // GROUP
+    own = [pl.ds(g * GROUP, GROUP) for g in range(groups)]
+    copies = [
+        pltpu.make_async_copy(sides, side, load.at[2 * groups]),
+        pltpu.make_async_copy(ends, end, load.at[2 * groups + 1]),
+    ]
+    planes, others = [], []
+    for g in range(groups):
+        begin = g * GROUP + (2 if g else 0)
+        some = pl.ds(begin, GROUP + (0 if g else 2))
+        planes.append(pltpu.make_async_copy(inner.at[some], sol.at[some], load.at[g]))
+        others.append(
+            [
+                pltpu.make_async_copy(right_side.at[own[g]], rhs.at[own[g]], load.at[groups + g]),
+                pltpu.make_async_copy(diagonal.at[own[g]], diag.at[own[g]], load.at[2 * groups + 2 + g]),
+            ]
+        )
+    for copy in copies + [planes[0]] + others[0]:
+        copy.start()
+    for g in range(1, groups):
+        for copy in [planes[g]] + others[g]:
+            copy.start()
+    for copy in copies:
+        copy.wait()
+    turned[...] = jnp.concatenate([side[...].reshape(DEEP, LANES), jnp.zeros((DEEP, LANES), f32)], axis=0).T
+    lane = lax.broadcasted_iota(jnp.int32, (ROWS, LANES), 1)
+
+    def plane(d, carry):
+        for t in range(4):
+            begin = t * ROWS
+            rows = pl.ds(begin, ROWS)
+            v = sol[d + 1, rows, :]
+            beside = sol[d, rows, :] + sol[d + 2, rows, :]
+            before = end[0, pl.ds(d, 1), :] if t == 0 else sol[d + 1, pl.ds(begin - 1, 1), :]
+            after = end[1, pl.ds(d, 1), :] if t == 3 else sol[d + 1, pl.ds(begin + ROWS, 1), :]
+            beside = beside + jnp.concatenate([before, v[:-1]], axis=0)
+            beside = beside + jnp.concatenate([v[1:], after], axis=0)
+            spot = t * SLAB + d
+            from_left = pltpu.roll(turned[pl.ds(0, ROWS), :], lax.rem(LANES - spot, LANES), 1)
+            from_right = pltpu.roll(turned[pl.ds(ROWS, ROWS), :], LANES - 1 - spot, 1)
+            beside = beside + jnp.where(lane == 0, from_left, pltpu.roll(v, 1, 1))
+            beside = beside + jnp.where(lane == LANES - 1, from_right, pltpu.roll(v, LANES - 1, 1))
+            res[d, rows, :] = rhs[d, rows, :] - ((6.0 + diag[d, rows, :]) * v - beside)
+        return carry
+
+    stores = []
+    for g in range(groups):
+        for copy in [planes[g]] + others[g]:
+            copy.wait()
+        lax.fori_loop(g * GROUP, (g + 1) * GROUP, plane, 0)
+        stores += [
+            pltpu.make_async_copy(res.at[own[g]], out_res.at[own[g]], store.at[0, g]),
+            pltpu.make_async_copy(
+                sol.at[pl.ds(g * GROUP + 1, GROUP)], out_sol.at[own[g]], store.at[1, g]
+            ),
+        ]
+        for copy in stores[-2:]:
+            copy.start()
+    for copy in stores:
+        copy.wait()
 
 
 def per_device(right_side, diagonal, regime, inverses):
@@ -368,18 +490,27 @@
     field = pltpu.VMEM((ROWS, DEEP, LANES), f32)
     padded = pltpu.VMEM((ROWS + 2, DEEP, LANES), f32)
     plane = (DEEP, LANES)
-    return pl.pallas_call(
+    anywhere = pl.BlockSpec(memory_space=pl.ANY)
+    wide = (SLAB + 2,) + right_side.shape[1:]
+    inner, sides, ends = pl.pallas_call(
         kernel,
-        out_shape=(shape, shape),
-        in_specs=[pl.BlockSpec(memory_space=pl.ANY)] * 4,
-        out_specs=[pl.BlockSpec(memory_space=pl.ANY)] * 2,
-        scratch_shapes=[field, field, padded, padded, padded] + [field] * 9 + [
+        out_shape=(
+            jax.ShapeDtypeStruct(wide, f32),
+            jax.ShapeDtypeStruct((4, SLAB, LANES), f32),
+            jax.ShapeDtypeStruct((2, SLAB, LANES), f32),
+        ),
+        in_specs=[anywhere] * 4,
+        out_specs=[anywhere] * 3,
+        scratch_shapes=[
+            field, field, padded, padded, padded, field, field, field, padded,
             pltpu.VMEM((ROWS, LANES), jnp.int32),
             pltpu.VMEM((NREG * DEEP, DEEP), f32),
             pltpu.VMEM((NREG * DEEP, 4 * DEEP), bf16),
             pltpu.VMEM((3, 2) + plane, f32),
             pltpu.VMEM((3,) + plane, f32),
             pltpu.VMEM((3,) + plane, f32),
+            pltpu.VMEM(plane, f32),
+            pltpu.VMEM(plane, f32),
             pltpu.VMEM((3, 4, 2, 8, LANES), f32),
             pltpu.VMEM((3, 4, 2, 8, LANES), f32),
             pltpu.VMEM((3, 8, 2, 8, LANES), f32),
@@ -390,13 +521,32 @@
             pltpu.SemaphoreType.DMA((3, 4)),
             pltpu.SemaphoreType.DMA((3, 3)),
             pltpu.SemaphoreType.DMA((3, 3)),
-            pltpu.SemaphoreType.DMA((2,)),
-            pltpu.SemaphoreType.DMA((2,)),
+            pltpu.SemaphoreType.DMA,
+            pltpu.SemaphoreType.DMA,
+            pltpu.SemaphoreType.DMA,
+            pltpu.SemaphoreType.DMA,
         ],
         compiler_params=pltpu.CompilerParams(
             collective_id=0, has_side_effects=True, vmem_limit_bytes=60 * 2**20
         ),
     )(right_side, diagonal, regime, inverses.reshape(NREG * DEEP, DEEP))
+    slab = pltpu.VMEM(right_side.shape, f32)
+    groups = SLAB // GROUP
+    return pl.pallas_call(
+        residual_kernel,
+        out_shape=(shape, shape),
+        in_specs=[anywhere] * 5,
+        out_specs=[anywhere] * 2,
+        scratch_shapes=[
+            pltpu.VMEM(wide, f32), slab, slab, slab,
+            pltpu.VMEM((4, SLAB, LANES), f32),
+            pltpu.VMEM((2, SLAB, LANES), f32),
+            pltpu.VMEM((LANES, LANES), f32),
+            pltpu.SemaphoreType.DMA((3 * groups + 2,)),
+            pltpu.SemaphoreType.DMA((2, groups)),
+        ],
+        compiler_params=pltpu.CompilerParams(vmem_limit_bytes=60 * 2**20),
+    )(right_side, diagonal, inner, sides, ends)
 
 
 def solution(mesh):

time: 158 us -> 130 us (0.82)
  Pallas kernels: 153 us -> 129 us
  local copies, waits for them, and re-layouts: 4.58 us -> 0 us
    pallas_call x1 -> x2, Pallas kernels: 153 us -> 129 us  [the longest x1 123 us: per_device(): pl.pallas_call(kernel, out_shape=(jax.ShapeDtypeStruct(wide, f32), jax.Sh...]
    unnamed x4 -> x0, local copies, waits for them, and re-layouts: 4.58 us -> none
where the time goes in v2:
time: 130 us; the launch traced here: 129 us
  Pallas kernels  129 us (99%)
    pallas_call x1, Pallas kernels, per_device(): pl.pallas_call(kernel, out_shape=(jax.ShapeDtypeStruct(wide, f32), jax.Sh...  123 us
    pallas_call x1, Pallas kernels, per_device(): pl.pallas_call(residual_kernel, out_shape=(shape, shape), in_specs=[anywh...  5.98 us

profile of v2, /device:TPU:1, one launch (start us, length us, event | category | flops | bytes accessed | tf_op | source)
XLA Modules:
  0.0 129.4 jit_solution(15309495684216871241)
XLA Ops:
  0.6 122.8 %shard_map.59 = (f32[18,256,128]{2,1,0:T(8,128)}, f32[4,16,128]{2,1,0:T(8,128)}, f32[2,16,128]{2,1,0:T(8,128)}) custom-call(f32[16,256,128]{2,1,0:T(8,128)} %right_side.3, f32[16,256,128]{2,1,0:T(8,128)} %diagonal.3, s32[256,128]{1,0:T(8,128)} %regime.1, f32[512,64]{1,0:T(8,128)} %bitcast.1), custom_call_target="tpu_custom_call" | custom-call | tf_op jit(solution)/shard_map/pallas_call | solution.py:495
  123.5 6.0 %shard_map.60 = (f32[16,256,128]{2,1,0:T(8,128)}, f32[16,256,128]{2,1,0:T(8,128)}) custom-call(f32[16,256,128]{2,1,0:T(8,128)} %right_side.3, f32[16,256,128]{2,1,0:T(8,128)} %diagonal.3, f32[18,256,128]{2,1,0:T(8,128)} %get-tuple-element.5.inner, f32[4,16,128]{2,1,0:T(8,128)} %get-tuple-element.6.sides, f32[2,16,128]{2,1,0:T(8,128)} %get-tuple-element.7.ends), custom_call_target="tpu_custom_call" | custom-call | tf_op jit(solution)/shard_map/pallas_call | solution.py:535

commit v3 on v2

--- a/solution.py
+++ b/solution.py
@@ -17,6 +17,8 @@
 LANES = 128
 CHUNK = 16
 STEPS = ROWS // CHUNK
+DEVICES = 128
+ORDER = (0, 3, 1, 2)
 UNROLL = 8
 GROUP = 4
 
@@ -37,8 +39,8 @@
 def kernel(
     right_side, diagonal, regime, blocks,
     out_sol, out_sides, out_ends,
-    res, diag, u0, m0, m1, w0, n0, w1, fin,
-    reg, inv, stack, edge, left, right, sides, blank, sum_a, sum_b, sum_c,
+    res, diag, u0, m0, m1, w0, n0, n1, w1, fin,
+    reg, inv, stack, edge, left, right, border, sides, blank, sums,
     col_sem, in_send, small_sem, halo_recv, halo_send, sum_recv, sum_send, out_recv, sides_recv, ends_recv, out_send,
 ):
     gx, gy, gz = lax.axis_index("gx"), lax.axis_index("gy"), lax.axis_index("gz")
@@ -52,12 +54,12 @@
     has_lower, has_upper = line > 0, line < 15
     has_left, has_right = gy > 0, gy < 7
 
-    def others(axis, me, count):
-        return [{axis: lax.rem(me + j, count)} for j in range(1, count)]
-
+    everyone = [
+        {"gx": lax.rem(gx + a, 4), "gy": lax.rem(gy + b, 8), "gz": lax.rem(gz + c, 4)}
+        for a in (2, 1, 3, 0) for b in (4, 3, 5, 2, 6, 1, 7, 0) for c in (2, 3, 1, 0)
+    ][:-1]
     barrier = pltpu.get_barrier_semaphore()
-    peers = others("gz", gz, 4) + others("gx", gx, 4) + others("gy", gy, 8)
-    for peer in peers:
+    for peer in everyone:
         pl.semaphore_signal(barrier, inc=1, device_id=peer, device_id_type=MESH)
 
     small = [
@@ -97,10 +99,10 @@
 
         lax.fori_loop(0, SLAB, body, 0)
 
-    pl.semaphore_wait(barrier, 13)
-    for c in range(STEPS):
+    pl.semaphore_wait(barrier, DEVICES - 1)
+    for c in ORDER:
         send_columns(0, right_side, res, c)
-    for c in range(STEPS // 2):
+    for c in ORDER[:2]:
         send_columns(1, diagonal, diag, c)
 
     nothing = jnp.zeros((DEEP, LANES), f32)
@@ -125,8 +127,7 @@
         def _():
             right[it] = nothing
 
-        edge[it, 0] = nothing
-        edge[it, 1] = nothing
+        edge[it] = nothing
 
     for copy in small:
         copy.wait()
@@ -136,7 +137,7 @@
     lane = lax.broadcasted_iota(jnp.int32, (DEEP, LANES), 1)
 
     def apply_blocks(source, target, it, c):
-        to_left, to_right = edge[it, 0], edge[it, 1]
+        ends = edge[it]
         for h in range(CHUNK // 2):
             x = c * CHUNK + 2 * h
             both = jnp.concatenate([source[x], source[x + 1]], axis=1)
@@ -155,11 +156,9 @@
             for j in range(2):
                 z = some[0][:, j * LANES : (j + 1) * LANES]
                 target[x + j + 1] = z
-                here = lane == x + j
-                to_left = jnp.where(here, pltpu.roll(z, x + j, 1), to_left)
-                to_right = jnp.where(here, pltpu.roll(z, x + j + 1, 1), to_right)
-        edge[it, 0] = to_left
-        edge[it, 1] = to_right
+                turned = pltpu.roll(z, 2 * (x + j) + 1, 1)
+                ends = jnp.where((lane == 2 * (x + j)) | (lane == 2 * (x + j) + 1), turned, ends)
+        edge[it] = ends
 
     def halo_copies(array, it):
         def copy(k, source, target, device):
@@ -168,57 +167,63 @@
                 device_id=device, device_id_type=MESH,
             )
 
+        copy = functools.partial(functools.partial, copy)
         return (
             (has_lower, has_upper, copy(0, array.at[1], array.at[ROWS + 1], lower)),
             (has_upper, has_lower, copy(1, array.at[ROWS], array.at[0], upper)),
-            (has_left, has_right, copy(2, edge.at[it, 0], right.at[it], {"gy": gy - 1})),
-            (has_right, has_left, copy(3, edge.at[it, 1], left.at[it], {"gy": gy + 1})),
+            (has_left, has_right, copy(2, edge.at[it], right.at[it], {"gy": gy - 1})),
+            (has_right, has_left, copy(3, edge.at[it], left.at[it], {"gy": gy + 1})),
         )
 
-    def start_halo(array, it):
-        for sends, _, copy in halo_copies(array, it):
-            pl.when(sends)(copy.start)
-
-    def wait_halo(array, it):
-        for _, receives, copy in halo_copies(array, it):
-            pl.when(receives)(copy.wait_recv)
-
-    def stencil(array, it, x):
+    def start_halo(array, it, which):
+        for sends, _, copy in halo_copies(array, it)[which]:
+            pl.when(sends)(lambda: copy().start())
+
+    def wait_halo(array, it, which):
+        for _, receives, copy in halo_copies(array, it)[which]:
+            pl.when(receives)(lambda: copy().wait_recv())
+
+    along_rows, along_lanes = slice(0, 2), slice(2, 4)
+    even = lax.rem(lane, 2) == 0
+    outer = (lane == 0) | (lane == LANES - 1)
+
+    def set_border(it):
+        border[...] = jnp.where(even, left[it], pltpu.roll(right[it], LANES - 2, 1))
+
+    def beyond(x):
+        turned = pltpu.roll(border[...], lax.rem(LANES - 2 * x, LANES), 1)
+        return jnp.where(outer, turned, 0.0)
+
+    def stencil(array, x):
         v = array[x + 1]
         beside = array[x] + array[x + 2]
         empty = jnp.zeros((1, LANES), f32)
         beside = beside + jnp.concatenate([empty, v[:-1]], axis=0)
         beside = beside + jnp.concatenate([v[1:], empty], axis=0)
-        from_left = pltpu.roll(left[it], lax.rem(LANES - x, LANES), 1)
-        from_right = pltpu.roll(right[it], LANES - 1 - x, 1)
-        beside = beside + jnp.where(lane == 0, from_left, pltpu.roll(v, 1, 1))
-        beside = beside + jnp.where(lane == LANES - 1, from_right, pltpu.roll(v, LANES - 1, 1))
+        beside = beside + jnp.where(lane == 0, 0.0, pltpu.roll(v, 1, 1))
+        beside = beside + jnp.where(lane == LANES - 1, 0.0, pltpu.roll(v, LANES - 1, 1))
         return v, (6.0 + diag[x]) * v - beside
 
-    sums = ((sum_a, "gz", gz, 4), (sum_b, "gx", gx, 4), (sum_c, "gy", gy, 8))
-
-    def start_sum(it, stage, value):
-        buffer, axis, me, count = sums[stage]
-        buffer[it, me] = value
-        for peer in others(axis, me, count):
+    me = (gx * 8 + gy) * 4 + gz
+    lower_half = lax.broadcasted_iota(jnp.int32, (1, LANES), 1) < LANES // 2
+
+    def start_sum(it, rz, wz):
+        rows = [jnp.sum(v, axis=0, keepdims=True) for v in (rz, wz)]
+        rows = [row + pltpu.roll(row, LANES // 2, 1) for row in rows]
+        sums[it, pl.ds(me, 1), :] = jnp.where(lower_half, rows[0], rows[1])
+        for peer in everyone:
             pltpu.make_async_remote_copy(
-                buffer.at[it, me], buffer.at[it, me], sum_send.at[it, stage], sum_recv.at[it, stage],
+                sums.at[it, me], sums.at[it, me], sum_send.at[it], sum_recv.at[it],
                 device_id=peer, device_id_type=MESH,
             ).start()
 
-    def end_sum(it, stage):
-        buffer, _, _, count = sums[stage]
-        some = buffer.at[it, pl.ds(0, count - 1)]
-        pltpu.make_async_copy(some, some, sum_recv.at[it, stage]).wait()
-        total = buffer[it, 0]
-        for k in range(1, count):
-            total = total + buffer[it, k]
-        return total
-
     def totals(it):
-        total = end_sum(it, 2)
-        whole = [jnp.sum(total[k], keepdims=True) for k in range(2)]
-        return [jnp.broadcast_to(t, (8, LANES)) for t in whole]
+        some = sums.at[it, pl.ds(0, DEVICES - 1)]
+        pltpu.make_async_copy(some, some, sum_recv.at[it]).wait()
+        total = jnp.sum(sums[it], axis=0, keepdims=True)
+        rz = jnp.sum(jnp.where(lower_half, total, 0.0), keepdims=True)
+        wz = jnp.sum(jnp.where(lower_half, 0.0, total), keepdims=True)
+        return [jnp.broadcast_to(v, (8, LANES)) for v in (rz, wz)]
 
     def folded(v):
         return jnp.sum(tiled(v), axis=0)
@@ -237,86 +242,101 @@
 
     zero = jnp.zeros((8, LANES), f32)
 
-    def first_precond(c, carry):
-        some = res.at[pl.ds(pl.multiple_of(c * CHUNK, CHUNK), CHUNK)]
-        pltpu.make_async_copy(some, some, col_sem.at[0, c]).wait()
-        apply_blocks(res, u0, 0, c)
-        return carry
-
-    lax.fori_loop(0, STEPS, first_precond, 0)
-    start_halo(u0, 0)
-    for c in range(STEPS // 2, STEPS):
+    def ordered(i):
+        return 3 * i - (i // 2) * (2 * i + 1)
+
+    def blocks_pass(it, source, target, before):
+        def body(i, carry):
+            c = ordered(i)
+            before(c)
+            apply_blocks(source, target, it, c)
+
+            @pl.when(i == 1)
+            def _():
+                start_halo(target, it, along_rows)
+
+            return carry
+
+        lax.fori_loop(0, STEPS, body, 0)
+        start_halo(target, it, along_lanes)
+
+    def arrived(array, target):
+        def wait(c):
+            some = target.at[pl.ds(pl.multiple_of(c * CHUNK, CHUNK), CHUNK)]
+            pltpu.make_async_copy(some, some, col_sem.at[array, c]).wait()
+
+        return wait
+
+    blocks_pass(0, res, u0, arrived(0, res))
+    for c in ORDER[2:]:
         send_columns(1, diagonal, diag, c)
-    wait_halo(u0, 0)
-
-    def first_image(c, carry):
-        some = diag.at[pl.ds(pl.multiple_of(c * CHUNK, CHUNK), CHUNK)]
-        pltpu.make_async_copy(some, some, col_sem.at[1, c]).wait()
+    wait_halo(u0, 0, along_rows)
+    wait_halo(u0, 0, along_lanes)
+    set_border(0)
+
+    def first_image(i, carry):
+        c = ordered(i)
+        arrived(1, diag)(c)
 
         def body(x, carry):
             rz, wz = carry
-            u, w = stencil(u0, 0, x)
+            u, w = stencil(u0, x)
+            w = w - beyond(x)
             w0[x] = w
             return rz + folded(res[x] * u), wz + folded(w * u)
 
         return rows_of(c, body, carry)
 
-    rz, wz = lax.fori_loop(0, STEPS, first_image, (zero, zero))
-
-    def blocks_beside_sum(it, source, target):
-        def body(c, carry):
-            apply_blocks(source, target, it + 1, c)
-            for stage in range(2):
-
-                @pl.when(c == 2 * stage)
-                def _():
-                    start_sum(it, stage + 1, end_sum(it, stage))
-
+    start_sum(0, *lax.fori_loop(0, STEPS, first_image, (zero, zero)))
+
+    def image_pass(it, array, target):
+        def body(x, carry):
+            _, target[x] = stencil(array, x)
             return carry
 
-        lax.fori_loop(0, STEPS, body, 0)
-
-    start_sum(0, 0, jnp.stack([rz, wz]))
-    blocks_beside_sum(0, w0, m0)
-    start_halo(m0, 1)
+        lax.fori_loop(CHUNK // UNROLL, (ROWS - CHUNK) // UNROLL, many(body), 0)
+        wait_halo(array, it, along_rows)
+        rows_of(0, body, 0)
+        rows_of(STEPS - 1, body, 0)
+
+    blocks_pass(1, w0, m0, lambda c: None)
+    image_pass(1, m0, n0)
+    wait_halo(m0, 1, along_lanes)
+    set_border(1)
     rz0, wz0 = totals(0)
     alpha0 = rz0 / wz0
-    wait_halo(m0, 1)
 
     def second(x, carry):
         rz, wz = carry
-        m, n = stencil(m0, 1, x)
+        n = n0[x] - beyond(x)
         n0[x] = n
         w = tiled(w0[x])
         r = tiled(res[x]) - alpha0 * w
-        u = tiled(u0[x + 1]) - alpha0 * tiled(m)
+        u = tiled(u0[x + 1]) - alpha0 * tiled(m0[x + 1])
         w = w - alpha0 * tiled(n)
         w1[x] = flat(w)
         return rz + jnp.sum(r * u, axis=0), wz + jnp.sum(w * u, axis=0)
 
-    rz, wz = lax.fori_loop(0, ROWS // UNROLL, many(second), (zero, zero))
-    start_sum(1, 0, jnp.stack([rz, wz]))
-    blocks_beside_sum(1, w1, m1)
-    start_halo(m1, 2)
+    start_sum(1, *lax.fori_loop(0, ROWS // UNROLL, many(second), (zero, zero)))
+    blocks_pass(2, w1, m1, lambda c: None)
+    image_pass(2, m1, n1)
+    wait_halo(m1, 2, along_lanes)
+    set_border(2)
     rz1, wz1 = totals(1)
     beta1 = rz1 / rz0
     alpha1 = rz1 / (wz1 - beta1 * rz1 / alpha0)
-    wait_halo(m1, 2)
 
     def third(x, carry):
         rz, wz = carry
-        m, n = stencil(m1, 2, x)
+        n = n1[x] - beyond(x)
         first_w, second_w = tiled(w0[x]), tiled(w1[x])
         r = tiled(res[x]) - alpha0 * first_w - alpha1 * (second_w + beta1 * first_w)
         second_m = tiled(m0[x + 1])
-        u = tiled(u0[x + 1]) - alpha0 * second_m - alpha1 * (tiled(m) + beta1 * second_m)
+        u = tiled(u0[x + 1]) - alpha0 * second_m - alpha1 * (tiled(m1[x + 1]) + beta1 * second_m)
         w = second_w - alpha1 * (tiled(n) + beta1 * tiled(n0[x]))
         return rz + jnp.sum(r * u, axis=0), wz + jnp.sum(w * u, axis=0)
 
-    rz, wz = lax.fori_loop(0, ROWS // UNROLL, many(third), (zero, zero))
-    start_sum(2, 0, jnp.stack([rz, wz]))
-    start_sum(2, 1, end_sum(2, 0))
-    start_sum(2, 2, end_sum(2, 1))
+    start_sum(2, *lax.fori_loop(0, ROWS // UNROLL, many(third), (zero, zero)))
     rz2, wz2 = totals(2)
     beta2 = rz2 / rz1
     alpha2 = rz2 / (wz2 - beta2 * rz2 / alpha1)
@@ -333,8 +353,7 @@
         return carry
 
     lax.fori_loop(0, (ROWS + 2) // 6, lambda i, k: [last_rows(6 * i + j, k) for j in range(6)][0], 0)
-    from_left, from_right = joined(left[0], left[1], left[2]), joined(right[0], right[1], right[2])
-    sides[...] = jnp.where(lane < ROWS, from_left, pltpu.roll(from_right, ROWS, 1))
+    sides[...] = joined(*[jnp.where(even, left[it], right[it]) for it in range(3)])
 
     mine = pl.ds(pl.multiple_of(part * ROWS, ROWS), ROWS)
     inner = fin.at[pl.ds(1, ROWS)]
@@ -398,10 +417,9 @@
         pltpu.make_async_copy(some, some, in_send.at[array]).wait()
     for it, array in enumerate((u0, m0, m1)):
         for sends, _, copy in halo_copies(array, it):
-            pl.when(sends)(copy.wait_send)
-        for stage, (buffer, _, _, count) in enumerate(sums):
-            group = buffer.at[it, pl.ds(0, count - 1)]
-            pltpu.make_async_copy(group, group, sum_send.at[it, stage]).wait()
+            pl.when(sends)(lambda: copy().wait_send())
+        group = sums.at[it, pl.ds(0, DEVICES - 1)]
+        pltpu.make_async_copy(group, group, sum_send.at[it]).wait()
     for target, recv in ((out_sides, sides_recv), (out_ends, ends_recv), (out_sol, out_recv)):
         pltpu.make_async_copy(target, target, recv).wait()
     pltpu.make_async_copy(some, some, out_send).wait()
@@ -421,7 +439,7 @@
 
 def residual_kernel(
     right_side, diagonal, inner, sides, ends, out_sol, out_res,
-    sol, rhs, diag, res, side, end, turned, load, store,
+    sol, rhs, diag, res, side, end, whole, turned, load, store,
 ):
     groups = SLAB // GROUP
     own = [pl.ds(g * GROUP, GROUP) for g in range(groups)]
@@ -447,7 +465,9 @@
             copy.start()
     for copy in copies:
         copy.wait()
-    turned[...] = jnp.concatenate([side[...].reshape(DEEP, LANES), jnp.zeros((DEEP, LANES), f32)], axis=0).T
+    whole[...] = jnp.concatenate([side[...].reshape(DEEP, LANES), jnp.zeros((DEEP, LANES), f32)], axis=0).T
+    for k in range(2):
+        turned[k] = whole[pl.ds(k, ROWS, stride=2), :]
     lane = lax.broadcasted_iota(jnp.int32, (ROWS, LANES), 1)
 
     def plane(d, carry):
@@ -461,8 +481,8 @@
             beside = beside + jnp.concatenate([before, v[:-1]], axis=0)
             beside = beside + jnp.concatenate([v[1:], after], axis=0)
             spot = t * SLAB + d
-            from_left = pltpu.roll(turned[pl.ds(0, ROWS), :], lax.rem(LANES - spot, LANES), 1)
-            from_right = pltpu.roll(turned[pl.ds(ROWS, ROWS), :], LANES - 1 - spot, 1)
+            from_left = pltpu.roll(turned[0], lax.rem(LANES - spot, LANES), 1)
+            from_right = pltpu.roll(turned[1], LANES - 1 - spot, 1)
             beside = beside + jnp.where(lane == 0, from_left, pltpu.roll(v, 1, 1))
             beside = beside + jnp.where(lane == LANES - 1, from_right, pltpu.roll(v, LANES - 1, 1))
             res[d, rows, :] = rhs[d, rows, :] - ((6.0 + diag[d, rows, :]) * v - beside)
@@ -502,25 +522,24 @@
         in_specs=[anywhere] * 4,
         out_specs=[anywhere] * 3,
         scratch_shapes=[
-            field, field, padded, padded, padded, field, field, field, padded,
+            field, field, padded, padded, padded, field, field, field, field, padded,
             pltpu.VMEM((ROWS, LANES), jnp.int32),
             pltpu.VMEM((NREG * DEEP, DEEP), f32),
             pltpu.VMEM((NREG * DEEP, 4 * DEEP), bf16),
-            pltpu.VMEM((3, 2) + plane, f32),
+            pltpu.VMEM((3,) + plane, f32),
             pltpu.VMEM((3,) + plane, f32),
             pltpu.VMEM((3,) + plane, f32),
             pltpu.VMEM(plane, f32),
             pltpu.VMEM(plane, f32),
-            pltpu.VMEM((3, 4, 2, 8, LANES), f32),
-            pltpu.VMEM((3, 4, 2, 8, LANES), f32),
-            pltpu.VMEM((3, 8, 2, 8, LANES), f32),
+            pltpu.VMEM(plane, f32),
+            pltpu.VMEM((3, DEVICES, LANES), f32),
             pltpu.SemaphoreType.DMA((2, STEPS)),
             pltpu.SemaphoreType.DMA((2,)),
             pltpu.SemaphoreType.DMA((2,)),
             pltpu.SemaphoreType.DMA((3, 4)),
             pltpu.SemaphoreType.DMA((3, 4)),
-            pltpu.SemaphoreType.DMA((3, 3)),
-            pltpu.SemaphoreType.DMA((3, 3)),
+            pltpu.SemaphoreType.DMA((3,)),
+            pltpu.SemaphoreType.DMA((3,)),
             pltpu.SemaphoreType.DMA,
             pltpu.SemaphoreType.DMA,
             pltpu.SemaphoreType.DMA,
@@ -542,6 +561,7 @@
             pltpu.VMEM((4, SLAB, LANES), f32),
             pltpu.VMEM((2, SLAB, LANES), f32),
             pltpu.VMEM((LANES, LANES), f32),
+            pltpu.VMEM((2, ROWS, LANES), f32),
             pltpu.SemaphoreType.DMA((3 * groups + 2,)),
             pltpu.SemaphoreType.DMA((2, groups)),
         ],

time: 130 us -> 119 us (0.915)
  Pallas kernels: 129 us -> 118 us
    pallas_call x1, Pallas kernels: 123 us -> 112 us  [per_device(): pl.pallas_call(kernel, out_shape=(jax.ShapeDtypeStruct(wide, f32), jax.Sh...]
where the time goes in v3:
time: 119 us
  Pallas kernels  118 us (99%)
    pallas_call x1, Pallas kernels, per_device(): pl.pallas_call(kernel, out_shape=(jax.ShapeDtypeStruct(wide, f32), jax.Sh...  112 us
    pallas_call x1, Pallas kernels, per_device(): pl.pallas_call(residual_kernel, out_shape=(shape, shape), in_specs=[anywh...  5.98 us

profile of v3, /device:TPU:1, one launch (start us, length us, event | category | flops | bytes accessed | tf_op | source)
XLA Modules:
  0.0 118.9 jit_solution(12719316250588785580)
XLA Ops:
  0.6 112.3 %shard_map.59 = (f32[18,256,128]{2,1,0:T(8,128)}, f32[4,16,128]{2,1,0:T(8,128)}, f32[2,16,128]{2,1,0:T(8,128)}) custom-call(f32[16,256,128]{2,1,0:T(8,128)} %right_side.3, f32[16,256,128]{2,1,0:T(8,128)} %diagonal.3, s32[256,128]{1,0:T(8,128)} %regime.1, f32[512,64]{1,0:T(8,128)} %bitcast.1), custom_call_target="tpu_custom_call" | custom-call | tf_op jit(solution)/shard_map/pallas_call | solution.py:515
  112.9 6.0 %shard_map.60 = (f32[16,256,128]{2,1,0:T(8,128)}, f32[16,256,128]{2,1,0:T(8,128)}) custom-call(f32[16,256,128]{2,1,0:T(8,128)} %right_side.3, f32[16,256,128]{2,1,0:T(8,128)} %diagonal.3, f32[18,256,128]{2,1,0:T(8,128)} %get-tuple-element.5.inner, f32[4,16,128]{2,1,0:T(8,128)} %get-tuple-element.6.sides, f32[2,16,128]{2,1,0:T(8,128)} %get-tuple-element.7.ends), custom_call_target="tpu_custom_call" | custom-call | tf_op jit(solution)/shard_map/pallas_call | solution.py:554

commit v4 on v3

--- a/solution.py
+++ b/solution.py
@@ -19,7 +19,7 @@
 STEPS = ROWS // CHUNK
 DEVICES = 128
 ORDER = (0, 3, 1, 2)
-UNROLL = 8
+UNROLL = 16
 GROUP = 4
 
 
@@ -41,7 +41,7 @@
     out_sol, out_sides, out_ends,
     res, diag, u0, m0, m1, w0, n0, n1, w1, fin,
     reg, inv, stack, edge, left, right, border, sides, blank, sums,
-    col_sem, in_send, small_sem, halo_recv, halo_send, sum_recv, sum_send, out_recv, sides_recv, ends_recv, out_send,
+    rounds, col_sem, in_send, small_sem, halo_recv, halo_send, sum_recv, sum_send, out_recv, sides_recv, ends_recv, out_send,
 ):
     gx, gy, gz = lax.axis_index("gx"), lax.axis_index("gy"), lax.axis_index("gz")
     odd = lax.rem(gx, 2)
@@ -59,8 +59,21 @@
         for a in (2, 1, 3, 0) for b in (4, 3, 5, 2, 6, 1, 7, 0) for c in (2, 3, 1, 0)
     ][:-1]
     barrier = pltpu.get_barrier_semaphore()
-    for peer in everyone:
-        pl.semaphore_signal(barrier, inc=1, device_id=peer, device_id_type=MESH)
+    layer, side, slot, core = gy // 2, lax.rem(gy, 2), gz // 2, lax.rem(gz, 2)
+    near_by = [{"gz": lax.rem(gz + j, 4)} for j in (1, 2, 3)]
+    near_by += [{"gx": lax.rem(gx + j, 4)} for j in (1, 3)]
+    near_by += [{"gy": lax.rem(gy + j, 8)} for j in (2, 6)]
+    near_by += [{"gy": 2 * layer + 1 - side, "gz": 2 * (1 - slot) + core}]
+
+    def tell(semaphore):
+        for peer in near_by:
+            pl.semaphore_signal(semaphore, inc=1, device_id=peer, device_id_type=MESH)
+
+    def spread(k):
+        tell(rounds.at[k])
+        pl.semaphore_wait(rounds.at[k], len(near_by))
+
+    tell(barrier)
 
     small = [
         pltpu.make_async_copy(blocks, inv, small_sem.at[0]),
@@ -99,7 +112,7 @@
 
         lax.fori_loop(0, SLAB, body, 0)
 
-    pl.semaphore_wait(barrier, DEVICES - 1)
+    pl.semaphore_wait(barrier, len(near_by))
     for c in ORDER:
         send_columns(0, right_side, res, c)
     for c in ORDER[:2]:
@@ -248,7 +261,7 @@
     def blocks_pass(it, source, target, before):
         def body(i, carry):
             c = ordered(i)
-            before(c)
+            before(i, c)
             apply_blocks(source, target, it, c)
 
             @pl.when(i == 1)
@@ -261,13 +274,18 @@
         start_halo(target, it, along_lanes)
 
     def arrived(array, target):
-        def wait(c):
+        def wait(i, c):
             some = target.at[pl.ds(pl.multiple_of(c * CHUNK, CHUNK), CHUNK)]
             pltpu.make_async_copy(some, some, col_sem.at[array, c]).wait()
 
         return wait
 
-    blocks_pass(0, res, u0, arrived(0, res))
+    def first_ready(i, c):
+        spread(i)
+        arrived(0, res)(i, c)
+
+    blocks_pass(0, res, u0, first_ready)
+    spread(STEPS)
     for c in ORDER[2:]:
         send_columns(1, diagonal, diag, c)
     wait_halo(u0, 0, along_rows)
@@ -276,7 +294,7 @@
 
     def first_image(i, carry):
         c = ordered(i)
-        arrived(1, diag)(c)
+        arrived(1, diag)(i, c)
 
         def body(x, carry):
             rz, wz = carry
@@ -299,7 +317,7 @@
         rows_of(0, body, 0)
         rows_of(STEPS - 1, body, 0)
 
-    blocks_pass(1, w0, m0, lambda c: None)
+    blocks_pass(1, w0, m0, lambda i, c: None)
     image_pass(1, m0, n0)
     wait_halo(m0, 1, along_lanes)
     set_border(1)
@@ -318,7 +336,7 @@
         return rz + jnp.sum(r * u, axis=0), wz + jnp.sum(w * u, axis=0)
 
     start_sum(1, *lax.fori_loop(0, ROWS // UNROLL, many(second), (zero, zero)))
-    blocks_pass(2, w1, m1, lambda c: None)
+    blocks_pass(2, w1, m1, lambda i, c: None)
     image_pass(2, m1, n1)
     wait_halo(m1, 2, along_lanes)
     set_border(2)
@@ -533,6 +551,7 @@
             pltpu.VMEM(plane, f32),
             pltpu.VMEM(plane, f32),
             pltpu.VMEM((3, DEVICES, LANES), f32),
+            pltpu.SemaphoreType.REGULAR((STEPS + 1,)),
             pltpu.SemaphoreType.DMA((2, STEPS)),
             pltpu.SemaphoreType.DMA((2,)),
             pltpu.SemaphoreType.DMA((2,)),

time: 119 us -> 116 us (0.975)
  Pallas kernels: 118 us -> 115 us
    pallas_call x1, Pallas kernels: 112 us -> 109 us  [per_device(): pl.pallas_call(kernel, out_shape=(jax.ShapeDtypeStruct(wide, f32), jax.Sh...]
where the time goes in v4:
time: 116 us
  Pallas kernels  115 us (99%)
    pallas_call x1, Pallas kernels, per_device(): pl.pallas_call(kernel, out_shape=(jax.ShapeDtypeStruct(wide, f32), jax.Sh...  109 us
    pallas_call x1, Pallas kernels, per_device(): pl.pallas_call(residual_kernel, out_shape=(shape, shape), in_specs=[anywh...  5.98 us

profile of v4, /device:TPU:1, one launch (start us, length us, event | category | flops | bytes accessed | tf_op | source)
XLA Modules:
  0.0 115.9 jit_solution(11874009988515008539)
XLA Ops:
  0.6 109.3 %shard_map.59 = (f32[18,256,128]{2,1,0:T(8,128)}, f32[4,16,128]{2,1,0:T(8,128)}, f32[2,16,128]{2,1,0:T(8,128)}) custom-call(f32[16,256,128]{2,1,0:T(8,128)} %right_side.3, f32[16,256,128]{2,1,0:T(8,128)} %diagonal.3, s32[256,128]{1,0:T(8,128)} %regime.1, f32[512,64]{1,0:T(8,128)} %bitcast.1), custom_call_target="tpu_custom_call" | custom-call | tf_op jit(solution)/shard_map/pallas_call | solution.py:533
  110.0 6.0 %shard_map.60 = (f32[16,256,128]{2,1,0:T(8,128)}, f32[16,256,128]{2,1,0:T(8,128)}) custom-call(f32[16,256,128]{2,1,0:T(8,128)} %right_side.3, f32[16,256,128]{2,1,0:T(8,128)} %diagonal.3, f32[18,256,128]{2,1,0:T(8,128)} %get-tuple-element.5.inner, f32[4,16,128]{2,1,0:T(8,128)} %get-tuple-element.6.sides, f32[2,16,128]{2,1,0:T(8,128)} %get-tuple-element.7.ends), custom_call_target="tpu_custom_call" | custom-call | tf_op jit(solution)/shard_map/pallas_call | solution.py:573

commit v5 on v4

--- a/solution.py
+++ b/solution.py
@@ -19,6 +19,7 @@
 STEPS = ROWS // CHUNK
 DEVICES = 128
 ORDER = (0, 3, 1, 2)
+EARLY = 16
 UNROLL = 16
 GROUP = 4
 
@@ -38,10 +39,10 @@
 
 def kernel(
     right_side, diagonal, regime, blocks,
-    out_sol, out_sides, out_ends,
+    out_sol, out_early, out_sides, out_ends, weights,
     res, diag, u0, m0, m1, w0, n0, n1, w1, fin,
     reg, inv, stack, edge, left, right, border, sides, blank, sums,
-    rounds, col_sem, in_send, small_sem, halo_recv, halo_send, sum_recv, sum_send, out_recv, sides_recv, ends_recv, out_send,
+    rounds, col_sem, in_send, small_sem, halo_recv, halo_send, sum_recv, sum_send, early_recv, early_send, out_recv, sides_recv, ends_recv, out_send,
 ):
     gx, gy, gz = lax.axis_index("gx"), lax.axis_index("gy"), lax.axis_index("gz")
     odd = lax.rem(gx, 2)
@@ -273,6 +274,61 @@
         lax.fori_loop(0, STEPS, body, 0)
         start_halo(target, it, along_lanes)
 
+    def give(k, source, target, send, recv):
+        pltpu.make_async_remote_copy(
+            source, target, send, recv, device_id={"gz": k}, device_id_type=MESH
+        ).start()
+
+    def keep(source, target, recv):
+        pltpu.make_async_copy(source, target, recv).start()
+
+    def deliver(source, target, pitch, offset, count, send, recv):
+        here = pl.ds(pl.multiple_of(part * pitch + offset, 8), count)
+
+        def plane(d, carry):
+            for j in range(1, 4):
+                k = lax.rem(gz + j, 4)
+                give(k, source.at[:, k * SLAB + d, :], target.at[d + 1, here, :], send, recv)
+            keep(source.at[:, base + d, :], target.at[d + 1, here, :], recv)
+            return carry
+
+        for j in range(1, 4):
+            k = lax.rem(gz + j, 4)
+
+            @pl.when(k > 0)
+            def _():
+                give(k, source.at[:, k * SLAB - 1, :], target.at[0, here, :], send, recv)
+
+            @pl.when(k < 3)
+            def _():
+                give(k, source.at[:, k * SLAB + SLAB, :], target.at[SLAB + 1, here, :], send, recv)
+
+        lax.fori_loop(0, SLAB, plane, 0)
+        for outside, plane_at, depth in ((gz == 0, 0, base - 1), (gz == 3, SLAB + 1, base + SLAB)):
+
+            @pl.when(jnp.logical_not(outside))
+            def _():
+                keep(source.at[:, depth, :], target.at[plane_at, here, :], recv)
+
+            @pl.when(outside)
+            def _():
+                for t in range(4):
+                    keep(blank.at[pl.ds(0, count)], target.at[plane_at, pl.ds(t * pitch + offset, count), :], recv)
+
+    def delivered(source, send):
+        some, one = source.at[:, pl.ds(0, 3 * SLAB), :], source.at[:, 0, :]
+        pltpu.make_async_copy(some, some, send).wait()
+        for _ in range(4):
+            pltpu.make_async_copy(one, one, send).wait()
+
+        @pl.when((gz == 0) | (gz == 3))
+        def _():
+            pltpu.make_async_copy(one, one, send).wait()
+
+    def early(it, array):
+        some = array.at[pl.ds(1, EARLY)]
+        deliver(some, out_early.at[it], EARLY, 0, EARLY, early_send.at[it], early_recv.at[it])
+
     def arrived(array, target):
         def wait(i, c):
             some = target.at[pl.ds(pl.multiple_of(c * CHUNK, CHUNK), CHUNK)]
@@ -318,6 +374,7 @@
         rows_of(STEPS - 1, body, 0)
 
     blocks_pass(1, w0, m0, lambda i, c: None)
+    early(0, u0)
     image_pass(1, m0, n0)
     wait_halo(m0, 1, along_lanes)
     set_border(1)
@@ -337,6 +394,7 @@
 
     start_sum(1, *lax.fori_loop(0, ROWS // UNROLL, many(second), (zero, zero)))
     blocks_pass(2, w1, m1, lambda i, c: None)
+    early(1, m0)
     image_pass(2, m1, n1)
     wait_halo(m1, 2, along_lanes)
     set_border(2)
@@ -355,6 +413,7 @@
         return rz + jnp.sum(r * u, axis=0), wz + jnp.sum(w * u, axis=0)
 
     start_sum(2, *lax.fori_loop(0, ROWS // UNROLL, many(third), (zero, zero)))
+    early(2, m1)
     rz2, wz2 = totals(2)
     beta2 = rz2 / rz1
     alpha2 = rz2 / (wz2 - beta2 * rz2 / alpha1)
@@ -362,6 +421,8 @@
     by_u = alpha0 + alpha1 * (1.0 + beta1) + alpha2 * (1.0 + beta2 * (1.0 + beta1))
     by_m = -alpha1 * alpha0 - alpha2 * (alpha0 + alpha1 * beta1 + beta2 * alpha0)
     by_n = -alpha2 * alpha1
+    for k, weight in enumerate((by_u, by_m, by_n)):
+        weights[k] = weight
 
     def joined(u, m, n):
         return flat(by_u * tiled(u) + by_m * tiled(m) + by_n * tiled(n))
@@ -373,62 +434,22 @@
     lax.fori_loop(0, (ROWS + 2) // 6, lambda i, k: [last_rows(6 * i + j, k) for j in range(6)][0], 0)
     sides[...] = joined(*[jnp.where(even, left[it], right[it]) for it in range(3)])
 
-    mine = pl.ds(pl.multiple_of(part * ROWS, ROWS), ROWS)
-    inner = fin.at[pl.ds(1, ROWS)]
-
-    def give(k, source, target, recv):
-        pltpu.make_async_remote_copy(
-            source, target, out_send, recv, device_id={"gz": k}, device_id_type=MESH
-        ).start()
-
-    def keep(source, target, recv):
-        pltpu.make_async_copy(source, target, recv).start()
-
+    late = fin.at[pl.ds(EARLY + 1, ROWS - EARLY)]
+    deliver(late, out_sol, ROWS, EARLY, ROWS - EARLY, out_send.at[0], out_recv)
     for j in range(1, 4):
         k = lax.rem(gz + j, 4)
         near = pl.ds(pl.multiple_of(k * SLAB, SLAB), SLAB)
-        give(k, sides.at[near], out_sides.at[part], sides_recv)
+        give(k, sides.at[near], out_sides.at[part], out_send.at[1], sides_recv)
         for end, here in enumerate((part == 0, part == 3)):
             row = end * (ROWS + 1)
-            pl.when(here)(functools.partial(give, k, fin.at[row, near], out_ends.at[end], ends_recv))
-
-        @pl.when(k > 0)
-        def _():
-            give(k, inner.at[:, k * SLAB - 1, :], out_sol.at[0, mine, :], out_recv)
-
-        @pl.when(k < 3)
-        def _():
-            give(k, inner.at[:, k * SLAB + SLAB, :], out_sol.at[SLAB + 1, mine, :], out_recv)
-
-    def send_back(d, carry):
-        for j in range(1, 4):
-            k = lax.rem(gz + j, 4)
-            give(k, inner.at[:, k * SLAB + d, :], out_sol.at[d + 1, mine, :], out_recv)
-        return carry
-
-    lax.fori_loop(0, SLAB, send_back, 0)
-
+            pl.when(here)(
+                functools.partial(give, k, fin.at[row, near], out_ends.at[end], out_send.at[2], ends_recv)
+            )
     near = pl.ds(base, SLAB)
     keep(sides.at[near], out_sides.at[part], sides_recv)
     for end, here in enumerate((part == 0, part == 3)):
         row = end * (ROWS + 1)
         pl.when(here)(functools.partial(keep, fin.at[row, near], out_ends.at[end], ends_recv))
-
-    def keep_own(d, carry):
-        keep(inner.at[:, base + d, :], out_sol.at[d + 1, mine, :], out_recv)
-        return carry
-
-    lax.fori_loop(0, SLAB, keep_own, 0)
-    for outside, plane, depth in ((gz == 0, 0, base - 1), (gz == 3, SLAB + 1, base + SLAB)):
-
-        @pl.when(jnp.logical_not(outside))
-        def _():
-            keep(inner.at[:, depth, :], out_sol.at[plane, mine, :], out_recv)
-
-        @pl.when(outside)
-        def _():
-            for k in range(4):
-                keep(blank, out_sol.at[plane, pl.ds(k * ROWS, ROWS), :], out_recv)
 
     some = res.at[pl.ds(0, 3 * SLAB)]
     for array in range(2):
@@ -438,55 +459,76 @@
             pl.when(sends)(lambda: copy().wait_send())
         group = sums.at[it, pl.ds(0, DEVICES - 1)]
         pltpu.make_async_copy(group, group, sum_send.at[it]).wait()
-    for target, recv in ((out_sides, sides_recv), (out_ends, ends_recv), (out_sol, out_recv)):
+    for it, array in enumerate((u0, m0, m1)):
+        delivered(array.at[pl.ds(1, EARLY)], early_send.at[it])
+        pltpu.make_async_copy(out_early.at[it], out_early.at[it], early_recv.at[it]).wait()
+    for target, recv in (
+        (out_sides, sides_recv),
+        (out_ends, ends_recv),
+        (out_sol.at[:, pl.ds(0, 4 * (ROWS - EARLY)), :], out_recv),
+    ):
         pltpu.make_async_copy(target, target, recv).wait()
-    pltpu.make_async_copy(some, some, out_send).wait()
-    pltpu.make_async_copy(sides.at[pl.ds(0, 3 * SLAB)], sides.at[pl.ds(0, 3 * SLAB)], out_send).wait()
-    for _ in range(4):
-        pltpu.make_async_copy(blank, blank, out_send).wait()
-
-    @pl.when(jnp.logical_or(gz == 0, gz == 3))
+    delivered(late, out_send.at[0])
+    some = sides.at[pl.ds(0, 3 * SLAB)]
+    pltpu.make_async_copy(some, some, out_send.at[1]).wait()
+
+    @pl.when((part == 0) | (part == 3))
     def _():
-        pltpu.make_async_copy(blank, blank, out_send).wait()
-
-    @pl.when(jnp.logical_or(part == 0, part == 3))
-    def _():
-        some_rows = blank.at[pl.ds(0, 3 * SLAB)]
-        pltpu.make_async_copy(some_rows, some_rows, out_send).wait()
+        pltpu.make_async_copy(some, some, out_send.at[2]).wait()
 
 
 def residual_kernel(
-    right_side, diagonal, inner, sides, ends, out_sol, out_res,
-    sol, rhs, diag, res, side, end, whole, turned, load, store,
+    right_side, diagonal, inner, terms, sides, ends, weights, out_sol, out_res,
+    sol, term, rhs, diag, res, side, end, spots, turned, load, store,
 ):
     groups = SLAB // GROUP
     own = [pl.ds(g * GROUP, GROUP) for g in range(groups)]
     copies = [
-        pltpu.make_async_copy(sides, side, load.at[2 * groups]),
-        pltpu.make_async_copy(ends, end, load.at[2 * groups + 1]),
+        pltpu.make_async_copy(sides, side, load.at[0, groups]),
+        pltpu.make_async_copy(ends, end, load.at[1, groups]),
     ]
     planes, others = [], []
     for g in range(groups):
         begin = g * GROUP + (2 if g else 0)
         some = pl.ds(begin, GROUP + (0 if g else 2))
-        planes.append(pltpu.make_async_copy(inner.at[some], sol.at[some], load.at[g]))
+        one = []
+        for t in range(4):
+            late = pl.ds(t * ROWS + EARLY, ROWS - EARLY)
+            one.append(pltpu.make_async_copy(inner.at[some, late], sol.at[some, late], load.at[t, g]))
+        for k in range(3):
+            one.append(pltpu.make_async_copy(terms.at[k, some], term.at[k, some], load.at[4 + k, g]))
+        planes.append(one)
         others.append(
             [
-                pltpu.make_async_copy(right_side.at[own[g]], rhs.at[own[g]], load.at[groups + g]),
-                pltpu.make_async_copy(diagonal.at[own[g]], diag.at[own[g]], load.at[2 * groups + 2 + g]),
+                pltpu.make_async_copy(right_side.at[own[g]], rhs.at[own[g]], load.at[7, g]),
+                pltpu.make_async_copy(diagonal.at[own[g]], diag.at[own[g]], load.at[8, g]),
             ]
         )
-    for copy in copies + [planes[0]] + others[0]:
+    for copy in copies:
         copy.start()
-    for g in range(1, groups):
-        for copy in [planes[g]] + others[g]:
+    for g in range(groups):
+        for copy in planes[g] + others[g]:
             copy.start()
     for copy in copies:
         copy.wait()
-    whole[...] = jnp.concatenate([side[...].reshape(DEEP, LANES), jnp.zeros((DEEP, LANES), f32)], axis=0).T
+    lane = lax.broadcasted_iota(jnp.int32, (ROWS, LANES), 1)
+    listed = side[...].reshape(DEEP, LANES)
     for k in range(2):
-        turned[k] = whole[pl.ds(k, ROWS, stride=2), :]
-    lane = lax.broadcasted_iota(jnp.int32, (ROWS, LANES), 1)
+        spots[pl.ds(k, DEEP, stride=2), :] = listed
+    spots[...] = spots[...].T
+    halves_of = [spots[pl.ds(k, ROWS, stride=2), :] for k in range(2)]
+    turned[...] = jnp.where(lax.rem(lane, 2) == 0, halves_of[0], pltpu.roll(halves_of[1], LANES - 2, 1))
+    outer = (lane == 0) | (lane == LANES - 1)
+
+    def join(d, carry):
+        for t in range(4):
+            rows = pl.ds(t * EARLY, EARLY)
+            parts = [
+                term[k, d, rows, :].reshape(EARLY // 8, 8, LANES) * weights[k] for k in range(3)
+            ]
+            total = parts[0] + parts[1] + parts[2]
+            sol[d, pl.ds(t * ROWS, EARLY), :] = total.reshape(EARLY, LANES)
+        return carry
 
     def plane(d, carry):
         for t in range(4):
@@ -499,17 +541,18 @@
             beside = beside + jnp.concatenate([before, v[:-1]], axis=0)
             beside = beside + jnp.concatenate([v[1:], after], axis=0)
             spot = t * SLAB + d
-            from_left = pltpu.roll(turned[0], lax.rem(LANES - spot, LANES), 1)
-            from_right = pltpu.roll(turned[1], LANES - 1 - spot, 1)
-            beside = beside + jnp.where(lane == 0, from_left, pltpu.roll(v, 1, 1))
-            beside = beside + jnp.where(lane == LANES - 1, from_right, pltpu.roll(v, LANES - 1, 1))
+            beyond = pltpu.roll(turned[...], lax.rem(LANES - 2 * spot, LANES), 1)
+            beside = beside + jnp.where(lane == 0, 0.0, pltpu.roll(v, 1, 1))
+            beside = beside + jnp.where(lane == LANES - 1, 0.0, pltpu.roll(v, LANES - 1, 1))
+            beside = beside + jnp.where(outer, beyond, 0.0)
             res[d, rows, :] = rhs[d, rows, :] - ((6.0 + diag[d, rows, :]) * v - beside)
         return carry
 
     stores = []
     for g in range(groups):
-        for copy in [planes[g]] + others[g]:
+        for copy in planes[g] + others[g]:
             copy.wait()
+        lax.fori_loop(g * GROUP + (2 if g else 0), (g + 1) * GROUP + 2, join, 0)
         lax.fori_loop(g * GROUP, (g + 1) * GROUP, plane, 0)
         stores += [
             pltpu.make_async_copy(res.at[own[g]], out_res.at[own[g]], store.at[0, g]),
@@ -530,15 +573,18 @@
     plane = (DEEP, LANES)
     anywhere = pl.BlockSpec(memory_space=pl.ANY)
     wide = (SLAB + 2,) + right_side.shape[1:]
-    inner, sides, ends = pl.pallas_call(
+    few = (3, SLAB + 2, 4 * EARLY, LANES)
+    inner, terms, sides, ends, weights = pl.pallas_call(
         kernel,
         out_shape=(
             jax.ShapeDtypeStruct(wide, f32),
+            jax.ShapeDtypeStruct(few, f32),
             jax.ShapeDtypeStruct((4, SLAB, LANES), f32),
             jax.ShapeDtypeStruct((2, SLAB, LANES), f32),
+            jax.ShapeDtypeStruct((3, 8, LANES), f32),
         ),
         in_specs=[anywhere] * 4,
-        out_specs=[anywhere] * 3,
+        out_specs=[anywhere] * 4 + [pl.BlockSpec(memory_space=pltpu.VMEM)],
         scratch_shapes=[
             field, field, padded, padded, padded, field, field, field, field, padded,
             pltpu.VMEM((ROWS, LANES), jnp.int32),
@@ -559,10 +605,12 @@
             pltpu.SemaphoreType.DMA((3, 4)),
             pltpu.SemaphoreType.DMA((3,)),
             pltpu.SemaphoreType.DMA((3,)),
+            pltpu.SemaphoreType.DMA((3,)),
+            pltpu.SemaphoreType.DMA((3,)),
             pltpu.SemaphoreType.DMA,
             pltpu.SemaphoreType.DMA,
             pltpu.SemaphoreType.DMA,
-            pltpu.SemaphoreType.DMA,
+            pltpu.SemaphoreType.DMA((3,)),
         ],
         compiler_params=pltpu.CompilerParams(
             collective_id=0, has_side_effects=True, vmem_limit_bytes=60 * 2**20
@@ -573,19 +621,19 @@
     return pl.pallas_call(
         residual_kernel,
         out_shape=(shape, shape),
-        in_specs=[anywhere] * 5,
+        in_specs=[anywhere] * 6 + [pl.BlockSpec(memory_space=pltpu.VMEM)],
         out_specs=[anywhere] * 2,
         scratch_shapes=[
-            pltpu.VMEM(wide, f32), slab, slab, slab,
+            pltpu.VMEM(wide, f32), pltpu.VMEM(few, f32), slab, slab, slab,
             pltpu.VMEM((4, SLAB, LANES), f32),
             pltpu.VMEM((2, SLAB, LANES), f32),
             pltpu.VMEM((LANES, LANES), f32),
-            pltpu.VMEM((2, ROWS, LANES), f32),
-            pltpu.SemaphoreType.DMA((3 * groups + 2,)),
+            pltpu.VMEM((ROWS, LANES), f32),
+            pltpu.SemaphoreType.DMA((9, groups + 1)),
             pltpu.SemaphoreType.DMA((2, groups)),
         ],
         compiler_params=pltpu.CompilerParams(vmem_limit_bytes=60 * 2**20),
-    )(right_side, diagonal, inner, sides, ends)
+    )(right_side, diagonal, inner, terms, sides, ends, weights)
 
 
 def solution(mesh):

time: 116 us -> 114 us (0.983)
  Pallas kernels: 115 us -> 113 us
    pallas_call x1, Pallas kernels: 109 us -> 107 us  [per_device(): pl.pallas_call(kernel, out_shape=(jax.ShapeDtypeStruct(wide, f32), jax.Sh...]
where the time goes in v5:
time: 114 us
  Pallas kernels  113 us (99%)
    pallas_call x1, Pallas kernels, per_device(): pl.pallas_call(kernel, out_shape=(jax.ShapeDtypeStruct(wide, f32), jax.Sh...  107 us
    pallas_call x1, Pallas kernels, per_device(): pl.pallas_call(residual_kernel, out_shape=(shape, shape), in_specs=[anywh...  6.84 us

profile of v5, /device:TPU:1, one launch (start us, length us, event | category | flops | bytes accessed | tf_op | source)
XLA Modules:
  0.0 114.0 jit_solution(341472615528789861)
XLA Ops:
  0.6 106.5 %shard_map.59 = (f32[18,256,128]{2,1,0:T(8,128)}, f32[3,18,64,128]{3,2,1,0:T(8,128)}, f32[4,16,128]{2,1,0:T(8,128)}, f32[2,16,128]{2,1,0:T(8,128)}, f32[3,8,128]{2,1,0:T(8,128)}) custom-call(f32[16,256,128]{2,1,0:T(8,128)} %right_side.3, f32[16,256,128]{2,1,0:T(8,128)} %diagonal.3, s32[256,128]{1,0:T(8,128)} %regime.1, f32[512,64]{1,0:T(8,128)} %bitcast.1), custom_call_target="tpu_custom_call" | custom-call | tf_op jit(solution)/shard_map/pallas_call | solution.py:577
  107.2 6.8 %shard_map.60 = (f32[16,256,128]{2,1,0:T(8,128)}, f32[16,256,128]{2,1,0:T(8,128)}) custom-call(f32[16,256,128]{2,1,0:T(8,128)} %right_side.3, f32[16,256,128]{2,1,0:T(8,128)} %diagonal.3, f32[18,256,128]{2,1,0:T(8,128)} %get-tuple-element.7.inner, f32[3,18,64,128]{3,2,1,0:T(8,128)} %get-tuple-element.8.terms, f32[4,16,128]{2,1,0:T(8,128)} %get-tuple-element.9.sides, ...), custom_call_target="tpu_custom_call" | custom-call | tf_op jit(solution)/shard_map/pallas_call | solution.py:621

commit v6 on v5

--- a/solution.py
+++ b/solution.py
@@ -242,10 +242,10 @@
     def folded(v):
         return jnp.sum(tiled(v), axis=0)
 
-    def many(body):
+    def many(body, count=UNROLL):
         def some(i, carry):
-            for j in range(UNROLL):
-                carry = body(i * UNROLL + j, carry)
+            for j in range(count):
+                carry = body(i * count + j, carry)
             return carry
 
         return some
@@ -368,7 +368,8 @@
             _, target[x] = stencil(array, x)
             return carry
 
-        lax.fori_loop(CHUNK // UNROLL, (ROWS - CHUNK) // UNROLL, many(body), 0)
+        for j in range(CHUNK, ROWS - CHUNK):
+            body(j, 0)
         wait_halo(array, it, along_rows)
         rows_of(0, body, 0)
         rows_of(STEPS - 1, body, 0)
@@ -412,7 +413,7 @@
         w = second_w - alpha1 * (tiled(n) + beta1 * tiled(n0[x]))
         return rz + jnp.sum(r * u, axis=0), wz + jnp.sum(w * u, axis=0)
 
-    start_sum(2, *lax.fori_loop(0, ROWS // UNROLL, many(third), (zero, zero)))
+    start_sum(2, *lax.fori_loop(0, ROWS // 8, many(third, 8), (zero, zero)))
     early(2, m1)
     rz2, wz2 = totals(2)
     beta2 = rz2 / rz1
@@ -435,7 +436,6 @@
     sides[...] = joined(*[jnp.where(even, left[it], right[it]) for it in range(3)])
 
     late = fin.at[pl.ds(EARLY + 1, ROWS - EARLY)]
-    deliver(late, out_sol, ROWS, EARLY, ROWS - EARLY, out_send.at[0], out_recv)
     for j in range(1, 4):
         k = lax.rem(gz + j, 4)
         near = pl.ds(pl.multiple_of(k * SLAB, SLAB), SLAB)
@@ -450,6 +450,8 @@
     for end, here in enumerate((part == 0, part == 3)):
         row = end * (ROWS + 1)
         pl.when(here)(functools.partial(keep, fin.at[row, near], out_ends.at[end], ends_recv))
+
+    deliver(late, out_sol, ROWS, EARLY, ROWS - EARLY, out_send.at[0], out_recv)
 
     some = res.at[pl.ds(0, 3 * SLAB)]
     for array in range(2):

time: 114 us -> 114 us (level)
  no operation moved by 1% of the time
where the time goes in v6:
time: 114 us
  Pallas kernels  113 us (99%)
    pallas_call x1, Pallas kernels, per_device(): pl.pallas_call(kernel, out_shape=(jax.ShapeDtypeStruct(wide, f32), jax.Sh...  106 us
    pallas_call x1, Pallas kernels, per_device(): pl.pallas_call(residual_kernel, out_shape=(shape, shape), in_specs=[anywh...  6.84 us

profile of v6, /device:TPU:1, one launch (start us, length us, event | category | flops | bytes accessed | tf_op | source)
XLA Modules:
  0.0 113.8 jit_solution(10958281679996030352)
XLA Ops:
  0.6 106.3 %shard_map.59 = (f32[18,256,128]{2,1,0:T(8,128)}, f32[3,18,64,128]{3,2,1,0:T(8,128)}, f32[4,16,128]{2,1,0:T(8,128)}, f32[2,16,128]{2,1,0:T(8,128)}, f32[3,8,128]{2,1,0:T(8,128)}) custom-call(f32[16,256,128]{2,1,0:T(8,128)} %right_side.3, f32[16,256,128]{2,1,0:T(8,128)} %diagonal.3, s32[256,128]{1,0:T(8,128)} %regime.1, f32[512,64]{1,0:T(8,128)} %bitcast.1), custom_call_target="tpu_custom_call" | custom-call | tf_op jit(solution)/shard_map/pallas_call | solution.py:579
  107.0 6.8 %shard_map.60 = (f32[16,256,128]{2,1,0:T(8,128)}, f32[16,256,128]{2,1,0:T(8,128)}) custom-call(f32[16,256,128]{2,1,0:T(8,128)} %right_side.3, f32[16,256,128]{2,1,0:T(8,128)} %diagonal.3, f32[18,256,128]{2,1,0:T(8,128)} %get-tuple-element.7.inner, f32[3,18,64,128]{3,2,1,0:T(8,128)} %get-tuple-element.8.terms, f32[4,16,128]{2,1,0:T(8,128)} %get-tuple-element.9.sides, ...), custom_call_target="tpu_custom_call" | custom-call | tf_op jit(solution)/shard_map/pallas_call | solution.py:623
